TPU v7x, 128 devices: a whole 4x4x4 slice. The times are simulated.
128 devices in a mesh: fsdp: 32 (over x, y, core), dp: 4 (over z).
Axes of the slice: x: 4, y: 4, z: 4, core: 2. Of those that a mesh axis runs over, the one named last changes fastest.
Arguments:
- tokens: bfloat16 [65536, 4096], P(('fsdp', 'dp')), may hold values from -40 to 40
- cotangent: bfloat16 [65536, 2048], P(('fsdp', 'dp')), may hold values from -20 to 20
- weight: bfloat16 [4096, 2048], P('fsdp'), may hold values from -1 to 1
- left_vector: float32 [4096], P('fsdp'), may hold values from -6 to 6
Outputs:
- layer_out: bfloat16 [65536, 2048], P(('fsdp', 'dp'))
- input_grad: bfloat16 [65536, 4096], P(('fsdp', 'dp'))
- update: bfloat16 [4096, 2048], P('fsdp')
- left_next: float32 [4096], P('fsdp')
- right_next: float32 [2048], replicated
All inputs are finite; a program needn't handle non-finite values.
Results may differ from a plain program's by a relative error of at most 0.015.
Values may be sent and summed in bfloat16 or wider, within the bound.
A program may use at most 128 MiB of HBM per device.

v0:
```python
import jax
import jax.numpy as jnp
from jax import lax
from jax.sharding import Mesh
from jax.sharding import PartitionSpec as P

FSDP = ("fsdp_0", "fsdp_1", "fsdp_2")
FSDP_DP = ("fsdp_0", "fsdp_1", "fsdp_2", "dp")


epsilon = 1e-06


def sent_to_all(value, axis):
    copies = jnp.broadcast_to(value, (lax.axis_size(axis), *value.shape))
    return lax.all_to_all(copies, axis, split_axis=0, concat_axis=0, tiled=True)


def taken_together(value, axis):
    return sent_to_all(value, axis).sum(axis=0)


def in_order(blocks, dim):
    blocks = jnp.moveaxis(blocks, 0, dim)
    dims = blocks.shape
    return blocks.reshape(*dims[:dim], dims[dim] * dims[dim + 1], *dims[dim + 2 :])


def gather_in_order(value, axes, order):
    blocks = value[None]
    for k in order:
        blocks = lax.all_gather(blocks, axes[k], axis=0, tiled=True)
    block = [lax.axis_size(axes[k]) for k in reversed(order)]
    blocks = blocks.reshape(*block, *value.shape)
    turned = sorted(range(len(order)), key=lambda place: order[len(order) - 1 - place])
    return blocks.transpose(*turned, *range(len(order), blocks.ndim)).reshape(-1, *value.shape)


def whole_of(value, axes, order, dim):
    return in_order(gather_in_order(value, axes, order), dim)


def over_copies(value, axis):
    everything = sent_to_all(value, axis)
    return jnp.sum(everything.astype(jnp.float32), axis=0)


def packed_total(arrays, axis):
    flat, at, done = (jnp.concatenate([a.reshape(-1) for a in arrays]), 0, [])
    running = taken_together(flat, axis)
    for a in arrays:
        done.append(running[at : at + a.size].reshape(a.shape))
        at += a.size
    return tuple(done)


def per_device(tokens, cotangent, weight, left_vector):
    weight_wide = weight.astype(jnp.float32)
    part_right = jnp.dot(left_vector, weight_wide)
    right_raw = taken_together(part_right, FSDP)
    right_next = right_raw / jnp.sqrt(jnp.sum(right_raw * right_raw) + epsilon)
    left_raw = jnp.dot(weight_wide, right_next)
    left_sq = taken_together(jnp.sum(left_raw * left_raw), FSDP)
    spectral = jnp.sqrt(left_sq + epsilon)
    left_next = left_raw / spectral
    gathered = whole_of(weight, (("fsdp_0", "fsdp_1"), "fsdp_2"), (0, 1), 0)
    product = jnp.dot(tokens, gathered, preferred_element_type=jnp.float32)
    layer_out = (product / spectral).astype(jnp.bfloat16)
    back_prod = lax.dot_general(
        cotangent, gathered, (((1,), (1,)), ((), ())), preferred_element_type=jnp.float32
    )
    input_grad = (back_prod / spectral).astype(jnp.bfloat16)
    shard_rows = weight.shape[0]
    shard_sum = lax.psum_scatter(
        lax.dot_general(
            tokens, cotangent, (((0,), (0,)), ((), ())), preferred_element_type=jnp.float32
        ).astype(jnp.bfloat16),
        FSDP,
        scatter_dimension=0,
        tiled=True,
    )
    grad_sum = over_copies(shard_sum, "dp").astype(jnp.float32)
    entry_count = shard_rows * lax.axis_size(FSDP) * weight.shape[1]
    along_right = jnp.dot(grad_sum, right_next)
    grad_sq_raw, inner_prod, cross_term = packed_total(
        (
            jnp.sum(grad_sum * grad_sum),
            jnp.sum(grad_sum * weight_wide),
            jnp.sum(left_next * along_right),
        ),
        FSDP,
    )
    rank_coeff = inner_prod / (spectral * spectral)
    gradient = grad_sum / spectral - rank_coeff * left_next[:, None] * right_next[None, :]
    left_unit = left_sq / (left_sq + epsilon)
    right_unit = jnp.sum(right_next * right_next)
    grad_sq = (
        grad_sq_raw / (spectral * spectral)
        - 2.0 * rank_coeff * cross_term / spectral
        + rank_coeff * rank_coeff * left_unit * right_unit
    )
    grad_rms = jnp.sqrt(grad_sq / entry_count + epsilon)
    update = (gradient / grad_rms).astype(jnp.bfloat16)
    return (layer_out, input_grad, update, left_next, right_next)


def solution(mesh):
    torus = Mesh(
        mesh.devices.reshape(4, 4, 2, mesh.shape["dp"]), ("fsdp_0", "fsdp_1", "fsdp_2", "dp")
    )
    placed = (P(FSDP_DP, None), P(FSDP_DP, None), P(FSDP, None), P(FSDP))
    return jax.shard_map(
        per_device,
        mesh=torus,
        in_specs=placed,
        out_specs=(P(FSDP_DP, None), P(FSDP_DP, None), P(FSDP, None), P(FSDP), P()),
        check_vma=False,
    )
```

profile of v0, /device:TPU:1, one launch (start us, length us, event | category | flops | bytes accessed | tf_op | source)
XLA Modules:
  0.0 247.7 jit_solution(5602320976544870512)
XLA Ops:
  8.0 0.0 copy-start
  8.0 0.0 all-gather.6.cloned.1.call-start
  8.1 0.7 all-gather.6.cloned.1.call-update
  8.7 0.0 reduce-scatter.2.cloned.1.call-start
  8.8 0.8 copy-done
  9.6 14.6 %convolution_convert_fusion = bf16[4096,2048]{1,0:T(8,128)(2,1)} fusion(bf16[512,4096]{1,0:T(8,128)(2,1)} %param.4, bf16[512,2048]{1,0:T(8,128)(2,1)S(1)} %copy-done), kind=kOutput, calls=%fused_computation | convolution fusion | flops 8598323200 | bytes 23068672 | tf_op jit(solution)/shard_map/dot_general | solution.py:75
  24.2 0.0 reduce-scatter.2.cloned.1.call-update
  24.2 0.0 all-gather.4.cloned.1.call-start
  24.3 60.4 %all-gather.6.cloned.1.call-done = bf16[2048,2048]{1,0:T(8,128)(2,1)} async-done(((bf16[128,2048]{1,0:T(8,128)(2,1)}), bf16[2048,2048]{1,0:T(8,128)(2,1)}) %all-gather.6.cloned.1.call-update) | async-done | bytes 8388624 | tf_op jit(solution)/shard_map/all_gather | solution.py:32
  84.7 0.0 copy-start.2
  84.7 0.0 copy-start.5
  84.7 0.0 all-gather.4.cloned.1.call-update
  84.7 1.0 copy-done.2
  85.7 0.0 copy-done.5
  85.7 0.2 fusion.6
  85.9 0.1 broadcast_in_dim.18
  86.1 17.9 %all_to_all.23 = f32[32,1,2048]{2,1,0:T(1,128)S(1)} all-to-all(f32[32,1,2048]{2,1,0:T(1,128)S(1)} %broadcast_in_dim.18), channel_id=1, replica_groups=mesh['fsdp_0'=4,'fsdp_1'=4,'fsdp_2'=2,'dp'=4] {'fsdp_0','fsdp_1','fsdp_2'}, dimensions={0} | all-to-all | bytes 524288 | tf_op jit(solution)/shard_map/all_to_all | solution.py:16
  103.9 0.2 reduce_sum.90
  104.1 0.6 multiply_reduce_fusion.3
  105.4 0.6 multiply_reduce_fusion.2
  106.0 0.0 copy-start.3
  106.0 0.8 multiply_reduce_fusion.4
  106.9 0.7 broadcast_in_dim.19
  107.5 10.9 %all_to_all.24 = f32[32,1,1]{2,1,0:T(1,128)S(1)} all-to-all(f32[32,1,1]{2,1,0:T(1,128)S(1)} %broadcast_in_dim.19), channel_id=1, replica_groups=mesh['fsdp_0'=4,'fsdp_1'=4,'fsdp_2'=2,'dp'=4] {'fsdp_0','fsdp_1','fsdp_2'}, dimensions={0} | all-to-all | bytes 256 | tf_op jit(solution)/shard_map/all_to_all | solution.py:16
  118.4 26.0 %reduce-scatter.2.cloned.1.call-done = bf16[128,2048]{1,0:T(8,128)(2,1)} async-done(((bf16[4096,2048]{1,0:T(8,128)(2,1)}), bf16[128,2048]{1,0:T(8,128)(2,1)}) %reduce-scatter.2.cloned.1.call-update) | async-done | bytes 524304 | tf_op jit(solution)/shard_map/reduce_scatter | solution.py:74
  144.4 2.6 %broadcast_in_dim.20 = bf16[4,128,2048]{2,1,0:T(8,128)(2,1)} broadcast(bf16[128,2048]{1,0:T(8,128)(2,1)} %reduce-scatter.2.cloned.1.call-done), dimensions={1,2} | broadcast | bytes 2621440 | tf_op jit(solution)/shard_map/broadcast_in_dim | solution.py:15
  147.0 4.4 %all-to-all-start.2 = ((bf16[4,128,2048]{2,1,0:T(8,128)(2,1)}), bf16[4,128,2048]{2,1,0:T(8,128)(2,1)}, u32[]{:S(2)}, u32[]{:S(2)}) async-start(bf16[4,128,2048]{2,1,0:T(8,128)(2,1)} %broadcast_in_dim.20), calls=%async_computation.3 | async-start | bytes 4194304 | tf_op jit(solution)/shard_map/all_to_all | solution.py:16
  151.5 0.7 reduce_sum.93
  152.8 0.0 copy-start.4
  152.8 23.0 %all-to-all-done.2 = bf16[4,128,2048]{2,1,0:T(8,128)(2,1)} async-done(((bf16[4,128,2048]{2,1,0:T(8,128)(2,1)}), bf16[4,128,2048]{2,1,0:T(8,128)(2,1)}, u32[]{:S(2)}, u32[]{:S(2)}) %all-to-all-start.2) | async-done | bytes 2097184 | tf_op jit(solution)/shard_map/all_to_all | solution.py:16
  175.8 2.1 convert_reduce_fusion
  177.9 0.9 fusion.1
  178.8 1.9 multiply_reduce_fusion.1
  180.7 1.9 pad_maximum_fusion
  182.6 0.6 broadcast_in_dim.21
  183.2 8.0 %all-to-all-start.3 = ((f32[32,1,3]{2,1,0:T(1,128)}), f32[32,1,3]{2,1,0:T(1,128)S(1)}, u32[]{:S(2)}, u32[]{:S(2)}) async-start(f32[32,1,3]{2,1,0:T(1,128)} %broadcast_in_dim.21), calls=%async_computation.4 | async-start | bytes 32768 | tf_op jit(solution)/shard_map/all_to_all | solution.py:16
  191.9 6.3 %all-to-all-done.3 = f32[32,1,3]{2,1,0:T(1,128)S(1)} async-done(((f32[32,1,3]{2,1,0:T(1,128)}), f32[32,1,3]{2,1,0:T(1,128)S(1)}, u32[]{:S(2)}, u32[]{:S(2)}) %all-to-all-start.3) | async-done | bytes 416 | tf_op jit(solution)/shard_map/all_to_all | solution.py:16
  198.1 0.1 reduce_sum.98
  198.2 0.6 fusion.5
  201.4 0.0 copy-done.3
  201.4 1.0 divide_convert_fusion.2
  202.4 8.3 %copy.16 = bf16[16,2,128,2048]{3,2,1,0:T(8,128)(2,1)S(1)} copy(bf16[16,2,128,2048]{3,2,0,1:T(8,128)(2,1)} %bitcast.45) | data formatting | bytes 33554432 | tf_op jit(solution)/shard_map/transpose | solution.py:36
  210.7 0.0 copy-done.4
  210.7 0.0 copy-start.1
  210.7 5.7 %copy-done.1 = bf16[16,2,128,2048]{3,2,1,0:T(8,128)(2,1)} copy-done((bf16[16,2,128,2048]{3,2,1,0:T(8,128)(2,1)}, bf16[16,2,128,2048]{3,2,1,0:T(8,128)(2,1)S(1)}, u32[]{:S(2)}) %copy-start.1) | copy-done | bytes 16777240
  216.4 0.0 copy-done.6
  216.4 10.1 %divide_convert_fusion.1 = bf16[512,2048]{1,0:T(8,128)(2,1)} fusion(bf16[512,4096]{1,0:T(8,128)(2,1)S(1)} %copy-done.6, bf16[4096,2048]{1,0:T(8,128)(2,1)S(1)} %bitcast.46, f32[]{:T(128)S(6)} %sqrt.10), kind=kOutput, calls=%fused_computation.3 | convolution fusion | flops 8592031744 | bytes 23068676 | tf_op jit(solution)/shard_map/dot_general | solution.py:67
  226.5 13.8 %divide_convert_fusion = bf16[512,4096]{1,0:T(8,128)(2,1)} fusion(bf16[512,2048]{1,0:T(8,128)(2,1)S(1)} %copy-done, bf16[4096,2048]{1,0:T(8,128)(2,1)} %bitcast.47, f32[]{:T(128)S(6)} %sqrt.10), kind=kOutput, calls=%fused_computation.1 | convolution fusion | flops 8594128896 | bytes 23068676 | tf_op jit(solution)/shard_map/dot_general | solution.py:69
  (4 shorter events, 0.0 us)
Async XLA Ops:
  8.0 1.6 copy-start
  8.0 76.7 %all-gather.6.cloned.1.call-start = ((), (), s32[]{:S(2)}) async-start(), calls=%async_computation.7 | async-start | bytes 8912896 | tf_op jit(solution)/shard_map/all_gather | solution.py:32
  8.7 135.7 %reduce-scatter.2.cloned.1.call-start = ((), (), s32[]{:S(2)}) async-start(), calls=%async_computation.6 | async-start | bytes 17301504 | tf_op jit(solution)/shard_map/reduce_scatter | solution.py:74
  24.2 178.2 %all-gather.4.cloned.1.call-start = ((), (), s32[]{:S(2)}) async-start(), calls=%async_computation.5 | async-start | bytes 25165824 | tf_op jit(solution)/shard_map/all_gather | solution.py:32
  84.7 1.0 copy-start.2
  84.7 1.0 copy-start.5
  106.0 95.4 %copy-start.3 = (f32[2048]{0:T(1024)}, f32[2048]{0:T(1024)S(1)}, u32[]{:S(2)}) copy-start(f32[2048]{0:T(1024)S(1)} %get-tuple-element.8) | copy-start | bytes 24580
  147.0 28.8 %all-to-all-start.2 = ((bf16[4,128,2048]{2,1,0:T(8,128)(2,1)}), bf16[4,128,2048]{2,1,0:T(8,128)(2,1)}, u32[]{:S(2)}, u32[]{:S(2)}) async-start(bf16[4,128,2048]{2,1,0:T(8,128)(2,1)} %broadcast_in_dim.20), calls=%async_computation.3 | async-start | bytes 4194304 | tf_op jit(solution)/shard_map/all_to_all | solution.py:16
  152.8 57.9 %copy-start.4 = (f32[128]{0:T(128)}, f32[128]{0:T(128)S(1)}, u32[]{:S(2)}) copy-start(f32[128]{0:T(128)S(1)} %broadcast_divide_fusion.1) | copy-start | bytes 1540
  183.2 14.9 %all-to-all-start.3 = ((f32[32,1,3]{2,1,0:T(1,128)}), f32[32,1,3]{2,1,0:T(1,128)S(1)}, u32[]{:S(2)}, u32[]{:S(2)}) async-start(f32[32,1,3]{2,1,0:T(1,128)} %broadcast_in_dim.21), calls=%async_computation.4 | async-start | bytes 32768 | tf_op jit(solution)/shard_map/all_to_all | solution.py:16
  202.4 14.0 %copy-start.6 = (bf16[512,4096]{1,0:T(8,128)(2,1)S(1)}, bf16[512,4096]{1,0:T(8,128)(2,1)}, u32[]{:S(2)}) copy-start(bf16[512,4096]{1,0:T(8,128)(2,1)} %param.4) | copy-start | bytes 12582916
  210.7 5.7 %copy-start.1 = (bf16[16,2,128,2048]{3,2,1,0:T(8,128)(2,1)}, bf16[16,2,128,2048]{3,2,1,0:T(8,128)(2,1)S(1)}, u32[]{:S(2)}) copy-start(bf16[16,2,128,2048]{3,2,1,0:T(8,128)(2,1)S(1)} %copy.16) | copy-start | bytes 50331652
Sparse Core Ops, SparseCore 0:
  11.0 73.6 all-gather.5
  86.3 33.1 all-gather.3
Sparse Core Ops, SparseCore 1:
  24.3 120.0 reduce-scatter.1
where the time goes:
time: 248 us
  waiting for transfers between devices  116 us (47%)
  matrix products  40.3 us (16%)
  blocking collectives  28.8 us (12%)
  local copies, waits for them, and re-layouts  20.4 us (8%)
  between operations  20.2 us (8%)
  starting transfers between devices  12.6 us (5%)
  other arithmetic  9.01 us (4%)
    all_gather x2, waiting for transfers between devices, gather_in_order(): blocks = lax.all_gather(blocks, axes[k], axis=0, tiled=True)  60.4 us
    all_to_all x2, waiting for transfers between devices, sent_to_all(): return lax.all_to_all(copies, axis, split_axis=0, concat_axis=0, tiled=True)  29.3 us
    all_to_all x2, blocking collectives, sent_to_all(): return lax.all_to_all(copies, axis, split_axis=0, concat_axis=0, tiled=True)  28.8 us
    reduce_scatter x1, waiting for transfers between devices, per_device(): lax.psum_scatter(lax.dot_general(tokens, cotangent, (((0,), (0,)), ((), (...  26 us
    dot_general x1, matrix products, per_device(): lax.dot_general(tokens, cotangent, (((0,), (0,)), ((), ())), preferred_el...  14.6 us
    dot_general x1, matrix products, per_device(): lax.dot_general(cotangent, gathered, (((1,), (1,)), ((), ())), preferred_...  13.8 us
    all_to_all x2, starting transfers between devices, sent_to_all(): return lax.all_to_all(copies, axis, split_axis=0, concat_axis=0, tiled=True)  12.5 us
    dot_general x1, matrix products, per_device(): product = jnp.dot(tokens, gathered, preferred_element_type=jnp.float32)  10.1 us
  transfers between devices with their start and end apart: 5, of which 4 were waited for; matrix products, arithmetic and copies ran while one was open for 12% of the time, Pallas kernels for 0%

commit v1 on v0

v1 whole, which is shorter than its diff:
```python
import jax
import jax.numpy as jnp
from jax import lax
from jax.experimental import pallas as pl
from jax.experimental.pallas import tpu as pltpu
from jax.sharding import Mesh
from jax.sharding import PartitionSpec as P

MESH = pl.DeviceIdType.MESH
BF, F32 = jnp.bfloat16, jnp.float32
EPS = 1e-06
ENTRIES = 4096 * 2048

FSDP = ("fx", "fy", "fc")
FSDP_DP = ("fx", "fy", "fc", "dp")
SIZE = {"fx": 4, "fy": 4, "fc": 2, "dp": 4}
ORDER = (("dp", "fx", "fy"), ("dp", "fy", "fx"), ("fx", "fy", "dp"), ("fy", "fx", "dp"))


def kernel(
    tok, cot, w, lv, lo, ig, up, ln_ref, rn_ref,
    W, T, TP, C, CP, D, R1, R2, E, Q1, Q2, F, R3, G, GA, LO, IG, UP,
    prc, prx, pry, sqc, sqx, sqy, nmc, nmx, nmy, nmz, scal,
    ag_s, ag_r, fw_s, fw_r, ex_s, ex_r, rs_s, rs_r, p3_s, p3_r, gz_s, gz_r,
    pr_s, pr_r, sq_s, sq_r, nm_s, nm_r, ld_w, ld_c, ld_t, st,
):
    pos = {name: lax.axis_index(name) for name in SIZE}
    mx, my, mc, mz = (pos[name] for name in ("fx", "fy", "fc", "dp"))
    oc = 1 - mc

    def peer(name, step):
        return {name: (pos[name] + step) % SIZE[name]}

    def copy_to(src, dst, s, r, dev):
        return pltpu.make_async_remote_copy(
            src_ref=src, dst_ref=dst, send_sem=s, recv_sem=r, device_id=dev, device_id_type=MESH
        )

    def arrived(dst, sem):
        pltpu.make_async_copy(dst, dst, sem).wait()

    sent = []

    def started(copy):
        copy.start()

    half = (pl.ds(0, 1024), pl.ds(1024, 1024))
    first, second = ("fx", "fy"), ("fy", "fx")

    def block(h, a1, a2, rows=slice(None)):
        xy = (a1, a2) if h == 0 else (a2, a1)
        return W.at[mc, xy[0], xy[1], rows, half[h]]

    top, bottom = pl.ds(0, 64), pl.ds(64, 64)
    gather = {}
    landed = {}
    for h in range(2):
        n1, n2 = first[h], second[h]
        m1, m2 = pos[n1], pos[n2]
        for op in range(5):
            if op == 0:
                name, at = n1, lambda step, rows=slice(None), h=h, m1=m1, m2=m2: block(h, (m1 + step) % 4, m2, rows)
            else:
                col = (m1 + (0, 3, 1, 2)[op - 1]) % 4
                name, at = n2, lambda step, rows=slice(None), h=h, col=col, m2=m2: block(h, col, (m2 + step) % 4, rows)
            plus, minus = peer(name, 1), peer(name, 3)
            src = (at(0), at(0), at(3, top), at(1, bottom))
            for e, dev in enumerate((plus, minus, plus, minus)):
                gather[h, op, e] = copy_to(src[e], src[e], ag_s.at[h, op, e], ag_r.at[h, op, e], dev)
            got = (at(3), at(1), at(2, top), at(2, bottom))
            for e in range(4):
                landed[h, op, e] = (got[e], ag_r.at[h, op, e])
    partner = peer("fc", 1)
    across, crossed = {}, {}
    for h in range(2):
        for slot in range(4):
            col = (pos[first[h]] + (0, 3, 1, 2)[slot]) % 4
            mine = W.at[mc, col, :, :, half[h]] if h == 0 else W.at[mc, :, col, :, half[h]]
            other = W.at[oc, col, :, :, half[h]] if h == 0 else W.at[oc, :, col, :, half[h]]
            across[h, slot] = copy_to(mine, mine, fw_s.at[h, slot], fw_r.at[h, slot], partner)
            crossed[h, slot] = (other, fw_r.at[h, slot])
    give_c = copy_to(C, CP, ex_s.at[4], ex_r.at[4], partner)
    give_t = [
        copy_to(T.at[oc, :, pl.ds(512 * g, 512)], TP.at[:, pl.ds(512 * g, 512)], ex_s.at[g], ex_r.at[g], partner)
        for g in range(4)
    ]

    ring = {}
    for ph, (S, A1, A2) in enumerate(((D, R1, R2), (E, Q1, Q2))):
        for k in range(4):
            name = ORDER[k][ph]
            m = pos[name]
            tp, tm, to = (m + 1) % 4, (m + 3) % 4, (m + 2) % 4
            plus, minus = peer(name, 1), peer(name, 3)
            a, b = pl.ds(0, 2), pl.ds(2, 2)
            moves = (
                (S.at[k, to, a], A1.at[k, 0], plus),
                (S.at[k, to, b], A1.at[k, 1], minus),
                (S.at[k, tp, b], A2.at[k, 0, b], plus),
                (S.at[k, tm, a], A2.at[k, 1, a], minus),
                (S.at[k, tp, a], A2.at[k, 0, a], plus),
                (S.at[k, tm, b], A2.at[k, 1, b], minus),
            )
            for e, (src, dst, dev) in enumerate(moves):
                ring[ph, k, e] = copy_to(src, dst, rs_s.at[ph, k, e], rs_r.at[ph, k, e], dev)
            ring[ph, k, "at"] = (m, tp, tm)
    last = {}
    for k in range(4):
        name = ORDER[k][2]
        for j in range(1, 4):
            to = (pos[name] + j) % 4
            last[k, j] = copy_to(F.at[k, to], R3.at[k, j - 1], p3_s.at[k, j - 1], p3_r.at[k, j - 1], {name: to})
    share = [
        copy_to(GA.at[mz], GA.at[mz], gz_s.at[j - 1], gz_r.at[j - 1], peer("dp", j)) for j in range(1, 4)
    ]

    def exchange(buf, name, s, r, base):
        m, n = pos[name], SIZE[name]
        return [
            (
                copy_to(buf.at[m], buf.at[m], s.at[base + j - 1], r.at[base + j - 1], peer(name, j)),
                buf.at[(m + n - j) % n],
                r.at[base + j - 1],
            )
            for j in range(1, n)
        ]

    small = {
        "pr0": exchange(prc, "fc", pr_s, pr_r, 0),
        "pr1": exchange(prx, "fx", pr_s, pr_r, 1),
        "pr2": exchange(pry, "fy", pr_s, pr_r, 4),
        "sq0": exchange(sqc, "fc", sq_s, sq_r, 0),
        "sq1": exchange(sqx, "fx", sq_s, sq_r, 1),
        "sq2": exchange(sqy, "fy", sq_s, sq_r, 4),
        "nm0": exchange(nmc, "fc", nm_s, nm_r, 0),
        "nm1": exchange(nmx, "fx", nm_s, nm_r, 1),
        "nm2": exchange(nmy, "fy", nm_s, nm_r, 4),
        "nm3": exchange(nmz, "dp", nm_s, nm_r, 7),
    }

    def put(key, buf, name, value):
        buf[pos[name]] = value
        for copy, _, _ in small[key]:
            copy.start()

    def total(key, buf):
        for _, dst, sem in small[key]:
            arrived(dst, sem)
        value = buf[0]
        for j in range(1, buf.shape[0]):
            value = value + buf[j]
        return value

    load_w = pltpu.make_async_copy(w, W.at[mc, mx, my], ld_w)
    load_w.start()
    load_c = pltpu.make_async_copy(cot, C, ld_c)
    load_c.start()
    for p in range(2):
        side = (oc + p) % 2
        for b in range(16):
            pltpu.make_async_copy(
                tok.at[:, pl.ds(pl.multiple_of((2 * b + side) * 128, 128), 128)],
                T.at[side, :, pl.ds(128 * b, 128)],
                ld_t.at[p, b // 4],
            ).start()

    def loaded(p, g):
        side = (oc + p) % 2
        region = T.at[side, :, pl.ds(512 * g, 512)]
        pltpu.make_async_copy(region, region, ld_t.at[p, g]).wait()

    barrier = pltpu.get_barrier_semaphore()
    for name, n in SIZE.items():
        for j in range(1, n):
            pl.semaphore_signal(barrier, inc=1, device_id=peer(name, j), device_id_type=MESH)
    pl.semaphore_wait(barrier, 10)

    load_w.wait()
    for h in range(2):
        for op in (0, 1):
            gather[h, op, 0].start()
            gather[h, op, 1].start()
    load_c.wait()
    give_c.start()
    w_wide = W[mc, mx, my].astype(F32)
    lv_col = jnp.broadcast_to(lv[...], (128, 128)).T[:, 0:1]
    put("pr0", prc, "fc", jnp.sum(w_wide * lv_col, axis=0, keepdims=True))
    for g in range(4):
        loaded(0, g)
        give_t[g].start()

    def forward(h, op):
        arrived(*landed[h, op, 0])
        gather[h, op, 2].start()
        arrived(*landed[h, op, 1])
        gather[h, op, 3].start()

    def spread(h, op):
        gather[h, op, 0].start()
        gather[h, op, 1].start()

    def cross(h, slot):
        arrived(*landed[h, slot + 1, 2])
        arrived(*landed[h, slot + 1, 3])
        across[h, slot].start()

    forward(0, 0)
    forward(1, 0)
    for op in (2, 3):
        for h in range(2):
            spread(h, op)

    def ring_go(ph, k, *events):
        for e in events:
            ring[ph, k, e].start()

    def ring_mid(ph, k):
        S, A1 = ((D, R1), (E, Q1))[ph]
        _, tp, tm = ring[ph, k, "at"]
        for d, (t, lo_, e) in enumerate(((tp, 0, 4), (tm, 2, 5))):
            arrived(A1.at[k, d], rs_r.at[ph, k, d])
            for i in range(2):
                S[k, t, lo_ + i] = (S[k, t, lo_ + i].astype(F32) + A1[k, d, i].astype(F32)).astype(BF)
            ring[ph, k, e].start()

    def ring_end(ph, k):
        S, A2, out = ((D, R2, E), (E, Q2, F))[ph]
        m = ring[ph, k, "at"][0]
        a, b = pl.ds(0, 2), pl.ds(2, 2)
        arrived(A2.at[k, 0, b], rs_r.at[ph, k, 2])
        arrived(A2.at[k, 1, a], rs_r.at[ph, k, 3])
        arrived(A2.at[k, 0, a], rs_r.at[ph, k, 4])
        arrived(A2.at[k, 1, b], rs_r.at[ph, k, 5])
        for i in range(4):
            out[k, i] = (
                S[k, m, i].astype(F32) + A2[k, 0, i].astype(F32) + A2[k, 1, i].astype(F32)
            ).astype(BF)

    arrived(CP, ex_r.at[4])
    for g in range(4):
        arrived(TP.at[:, pl.ds(512 * g, 512)], ex_r.at[g])
        loaded(1, g)

    over_tokens = (((0,), (0,)), ((), ()))

    def pr_step1():
        put("pr1", prx, "fx", total("pr0", prc))

    def pr_step2():
        put("pr2", pry, "fy", total("pr1", prx))

    def term(i, carry):
        turn = i // 4
        x = i % 4
        q = (mz + 6 - turn) % 4
        cs = pl.ds(pl.multiple_of(q * 512, 512), 512)
        ms = pl.ds(pl.multiple_of(x * 512, 512), 512)
        r = lax.dot_general(T[mc, :, ms], C[:, cs], over_tokens, preferred_element_type=F32)
        r = r + lax.dot_general(TP[:, ms], CP[:, cs], over_tokens, preferred_element_type=F32)
        r = r.astype(BF)
        for y in range(4):
            rows = slice(128 * y, 128 * y + 128)
            D[0, q, x, y] = r[rows, 0:128]
            D[1, q, y, x] = r[rows, 128:256]
            D[2, x, y, q] = r[rows, 256:384]
            D[3, y, x, q] = r[rows, 384:512]

        @pl.when(i == 3)
        def _():
            for k in (0, 1):
                ring_go(0, k, 0, 1)
            pr_step1()
            forward(0, 1)
            forward(1, 1)

        @pl.when(i == 7)
        def _():
            for k in (0, 1):
                ring_go(0, k, 2)
            for h in range(2):
                arrived(*landed[h, 0, 2])
                arrived(*landed[h, 0, 3])
                spread(h, 4)

        @pl.when(i == 11)
        def _():
            pr_step2()

        return carry

    lax.fori_loop(0, 16, term, 0)
    for k in (0, 1):
        ring_go(0, k, 3)
    for k in (2, 3):
        ring_go(0, k, 0, 1, 2, 3)
    for op in (2, 3):
        for h in range(2):
            forward(h, op)

    right_raw = total("pr2", pry)
    right_next = right_raw / jnp.sqrt(jnp.sum(right_raw * right_raw) + EPS)
    rn_ref[...] = right_next
    left_raw = jnp.sum(W[mc, mx, my].astype(F32) * right_next, axis=1, keepdims=True)
    put("sq0", sqc, "fc", jnp.broadcast_to(jnp.sum(left_raw * left_raw, keepdims=True), (8, 128)))

    ring_mid(0, 0)
    ring_mid(0, 1)
    put("sq1", sqx, "fx", total("sq0", sqc))
    for h in range(2):
        forward(h, 4)
        cross(h, 0)
    put("sq2", sqy, "fy", total("sq1", sqx))
    for h in range(2):
        cross(h, 1)
        cross(h, 2)
    ring_mid(0, 2)
    ring_mid(0, 3)
    for k in (0, 1):
        ring_end(0, k)
        ring_go(1, k, 0, 1, 2, 3)
    left_sq = total("sq2", sqy)
    scal[0] = left_sq
    scal[1] = 1.0 / jnp.sqrt(left_sq + EPS)
    for h in range(2):
        cross(h, 3)
    for h in range(2):
        for slot in range(4):
            arrived(*crossed[h, slot])

    inv = scal[1][0:1, 0:1]

    def back(i, carry):
        x, p = i // 2, i % 2
        rows = W[p, x].reshape(512, 2048)
        r = lax.dot_general(C[...], rows, (((1,), (1,)), ((), ())), preferred_element_type=F32)
        r = (r * inv).astype(BF)
        for y in range(4):
            at = pl.multiple_of(((x * 4 + y) * 2 + p) * 128, 128)
            IG[:, pl.ds(at, 128)] = r[:, 128 * y : 128 * y + 128]

        @pl.when(p == 1)
        def _():
            cs = pl.ds(pl.multiple_of(x * 1024, 1024), 1024)
            pltpu.make_async_copy(IG.at[:, cs], ig.at[:, cs], st.at[0]).start()

        @pl.when(i == 2)
        def _():
            for k in (2, 3):
                ring_end(0, k)
                ring_go(1, k, 0, 1, 2, 3)

        @pl.when(i == 4)
        def _():
            for k in (0, 1):
                ring_mid(1, k)

        @pl.when(i == 6)
        def _():
            for k in (2, 3):
                ring_mid(1, k)

        return carry

    lax.fori_loop(0, 8, back, 0)

    def p3_go(k):
        for j in range(1, 4):
            last[k, j].start()

    def front(i, carry):
        cs = pl.ds(pl.multiple_of(i * 256, 256), 256)
        r = jnp.dot(T[0], W[0, :, :, :, cs].reshape(2048, 256), preferred_element_type=F32)
        r = r + jnp.dot(T[1], W[1, :, :, :, cs].reshape(2048, 256), preferred_element_type=F32)
        LO[:, cs] = (r * inv).astype(BF)
        pltpu.make_async_copy(LO.at[:, cs], lo.at[:, cs], st.at[1]).start()

        @pl.when(i == 0)
        def _():
            for k in (0, 1):
                ring_end(1, k)
                p3_go(k)

        @pl.when(i == 2)
        def _():
            for k in (2, 3):
                ring_end(1, k)
                p3_go(k)

        @pl.when(i == 4)
        def _():
            quarter = pl.ds(pl.multiple_of(mz * 512, 512), 512)
            rn = rn_ref[:, quarter]
            wq = W[mc, mx, my, :, quarter].astype(F32)
            raw = jnp.sum(W[mc, mx, my].astype(F32) * rn_ref[...], axis=1, keepdims=True)
            ln = raw * inv
            sums = [jnp.zeros((1, 128), F32)] * 3
            for k in range(4):
                g = F[k, pos[ORDER[k][2]]].astype(F32)
                for j in range(3):
                    arrived(R3.at[k, j], p3_r.at[k, j])
                    g = g + R3[k, j].astype(F32)
                cols = slice(128 * k, 128 * k + 128)
                GA[mz, :, cols] = g.astype(BF)
                sums[0] = sums[0] + jnp.sum(g * g, axis=0, keepdims=True)
                sums[1] = sums[1] + jnp.sum(g * wq[:, cols], axis=0, keepdims=True)
                sums[2] = sums[2] + jnp.sum(g * ln, axis=0, keepdims=True) * rn[:, cols]
            for copy in share:
                copy.start()
            put("nm0", nmc, "fc", jnp.concatenate(sums + [jnp.zeros((5, 128), F32)], axis=0))

        @pl.when(i == 5)
        def _():
            put("nm1", nmx, "fx", total("nm0", nmc))

        @pl.when(i == 6)
        def _():
            put("nm2", nmy, "fy", total("nm1", nmx))

        return carry

    lax.fori_loop(0, 8, front, 0)
    put("nm3", nmz, "dp", total("nm2", nmy))

    sums = jnp.sum(total("nm3", nmz), axis=1, keepdims=True)
    grad_sq_raw, inner, crossed_term = sums[0:1], sums[1:2], sums[2:3]
    lsq = scal[0][0:1, 0:1]
    sq = lsq + EPS
    coeff = inner / sq
    rn = rn_ref[...]
    raw = jnp.sum(W[mc, mx, my].astype(F32) * rn, axis=1, keepdims=True)
    ln = raw * inv
    ln_ref[...] = jnp.broadcast_to(ln, (128, 128)).T[0:1]
    right_unit = jnp.sum(rn * rn, keepdims=True)
    grad_sq = (
        grad_sq_raw / sq - 2.0 * coeff * crossed_term * inv + coeff * coeff * (lsq / sq) * right_unit
    )
    inv_rms = 1.0 / jnp.sqrt(grad_sq / ENTRIES + EPS)
    for j in range(1, 4):
        arrived(GA.at[(mz + 4 - j) % 4], gz_r.at[j - 1])
    scale = inv * inv_rms
    column = ln * (coeff * inv_rms)
    for q in range(4):
        cs = slice(512 * q, 512 * q + 512)
        UP[:, cs] = (GA[q].astype(F32) * scale - column * rn[:, cs]).astype(BF)
    put_up = pltpu.make_async_copy(UP, up, st.at[2])
    put_up.start()

    for copy in gather.values():
        copy.wait_send()
    for copy in across.values():
        copy.wait_send()
    give_c.wait_send()
    for copy in give_t:
        copy.wait_send()
    for key, copy in ring.items():
        if key[2] != "at":
            copy.wait_send()
    for copy in last.values():
        copy.wait_send()
    for copy in share:
        copy.wait_send()
    for copies in small.values():
        for copy, _, _ in copies:
            copy.wait_send()
    pltpu.make_async_copy(IG, ig, st.at[0]).wait()
    pltpu.make_async_copy(LO, lo, st.at[1]).wait()
    put_up.wait()


def per_device(tokens, cotangent, weight, left_vector):
    dma = pltpu.SemaphoreType.DMA
    vm = pltpu.VMEM
    hbm = pl.BlockSpec(memory_space=pl.ANY)
    vmem = pl.BlockSpec(memory_space=pltpu.VMEM)
    unit = (128, 128)
    outs = pl.pallas_call(
        kernel,
        out_shape=(
            jax.ShapeDtypeStruct((512, 2048), BF),
            jax.ShapeDtypeStruct((512, 4096), BF),
            jax.ShapeDtypeStruct((128, 2048), BF),
            jax.ShapeDtypeStruct((1, 128), F32),
            jax.ShapeDtypeStruct((1, 2048), F32),
        ),
        in_specs=[hbm, hbm, hbm, vmem],
        out_specs=(hbm, hbm, hbm, vmem, vmem),
        scratch_shapes=[
            vm((2, 4, 4, 128, 2048), BF),
            vm((2, 512, 2048), BF),
            vm((512, 2048), BF),
            vm((512, 2048), BF),
            vm((512, 2048), BF),
            vm((4, 4, 4, 4, *unit), BF),
            vm((4, 2, 2, 4, *unit), BF),
            vm((4, 2, 4, 4, *unit), BF),
            vm((4, 4, 4, *unit), BF),
            vm((4, 2, 2, *unit), BF),
            vm((4, 2, 4, *unit), BF),
            vm((4, 4, *unit), BF),
            vm((4, 3, *unit), BF),
            vm((8, 128), F32),
            vm((4, 128, 512), BF),
            vm((512, 2048), BF),
            vm((512, 4096), BF),
            vm((128, 2048), BF),
            vm((2, 1, 2048), F32),
            vm((4, 1, 2048), F32),
            vm((4, 1, 2048), F32),
            vm((2, 8, 128), F32),
            vm((4, 8, 128), F32),
            vm((4, 8, 128), F32),
            vm((2, 8, 128), F32),
            vm((4, 8, 128), F32),
            vm((4, 8, 128), F32),
            vm((4, 8, 128), F32),
            vm((2, 8, 128), F32),
            dma((2, 5, 4)),
            dma((2, 5, 4)),
            dma((2, 4)),
            dma((2, 4)),
            dma((5,)),
            dma((5,)),
            dma((2, 4, 6)),
            dma((2, 4, 6)),
            dma((4, 3)),
            dma((4, 3)),
            dma((3,)),
            dma((3,)),
            dma((7,)),
            dma((7,)),
            dma((7,)),
            dma((7,)),
            dma((10,)),
            dma((10,)),
            dma,
            dma,
            dma((2, 4)),
            dma((3,)),
        ],
        compiler_params=pltpu.CompilerParams(
            collective_id=0, has_side_effects=True, vmem_limit_bytes=62 * 2**20
        ),
    )(tokens, cotangent, weight, left_vector.reshape(1, 128))
    layer_out, input_grad, update, left_next, right_next = outs
    return (layer_out, input_grad, update, left_next.reshape(128), right_next.reshape(2048))


def solution(mesh):
    torus = Mesh(mesh.devices.reshape(4, 4, 2, mesh.shape["dp"]), FSDP_DP)
    return jax.shard_map(
        per_device,
        mesh=torus,
        in_specs=(P(FSDP_DP, None), P(FSDP_DP, None), P(FSDP, None), P(FSDP)),
        out_specs=(P(FSDP_DP, None), P(FSDP_DP, None), P(FSDP, None), P(FSDP), P()),
        check_vma=False,
    )
```

time: 248 us -> 117 us (0.47)
  waiting for transfers between devices: 116 us -> 0 us
  Pallas kernels: 0 us -> 108 us
  matrix products: 40.3 us -> 0 us
  blocking collectives: 28.8 us -> 0 us
  between operations: 20.2 us -> 0.66 us
  local copies, waits for them, and re-layouts: 20.4 us -> 7.24 us
  starting transfers between devices: 12.6 us -> 0 us
  other arithmetic: 9.01 us -> 0 us
    pallas_call x0 -> x1, Pallas kernels: none -> 108 us  [per_device(): pl.pallas_call(kernel, out_shape=(jax.ShapeDtypeStruct((512, 2048), BF),...]
    all_gather x2 -> x0, waiting for transfers between devices: 60.4 us -> none  [gather_in_order(): blocks = lax.all_gather(blocks, axes[k], axis=0, tiled=True)]
    dot_general x6 -> x0, matrix products: 40.3 us -> none  [the longest x1 14.6 us: per_device(): lax.dot_general(tokens, cotangent, (((0,), (0,)), ((), ())), preferred_el...]
    all_to_all x2 -> x0, waiting for transfers between devices: 29.3 us -> none  [sent_to_all(): return lax.all_to_all(copies, axis, split_axis=0, concat_axis=0, tiled=True)]
    all_to_all x2 -> x0, blocking collectives: 28.8 us -> none  [sent_to_all(): return lax.all_to_all(copies, axis, split_axis=0, concat_axis=0, tiled=True)]
    reduce_scatter x1 -> x0, waiting for transfers between devices: 26 us -> none  [per_device(): lax.psum_scatter(lax.dot_general(tokens, cotangent, (((0,), (0,)), ((), (...]
    all_to_all x2 -> x0, starting transfers between devices: 12.5 us -> none  [sent_to_all(): return lax.all_to_all(copies, axis, split_axis=0, concat_axis=0, tiled=True)]
    transpose x1 -> x0, local copies, waits for them, and re-layouts: 8.26 us -> none  [gather_in_order(): blocks.transpose(*turned, *range(len(order), blocks.ndim))]
  transfers between devices with their start and end apart: 5 -> 0, of which waited for: 4 -> 0; matrix products, arithmetic and copies ran while one was open for 12% -> 0% of each run, Pallas kernels for 0% -> 0%
where the time goes in v1:
time: 117 us; the launch traced here: 116 us
  Pallas kernels  108 us (92%)
  local copies, waits for them, and re-layouts  7.24 us (6%)
    pallas_call x1, Pallas kernels, per_device(): pl.pallas_call(kernel, out_shape=(jax.ShapeDtypeStruct((512, 2048), BF),...  108 us
    unnamed x13, local copies, waits for them, and re-layouts  7.24 us

profile of v1, /device:TPU:1, one launch (start us, length us, event | category | flops | bytes accessed | tf_op | source)
XLA Modules:
  0.0 116.0 jit_solution(4406807015160934770)
XLA Ops:
  0.6 108.1 %shard_map.83 = (bf16[512,2048]{1,0:T(8,128)(2,1)}, bf16[512,4096]{1,0:T(8,128)(2,1)}, bf16[128,2048]{1,0:T(8,128)(2,1)}, f32[1,128]{1,0:T(1,128)}, f32[1,2048]{1,0:T(1,128)}) custom-call(bf16[512,4096]{1,0:T(8,128)(2,1)} %tok.1, bf16[512,2048]{1,0:T(8,128)(2,1)} %cot.1, bf16[128,2048]{1,0:T(8,128)(2,1)} %w.1, f32[1,128]{1,0:T(1,128)} %bitcast.4), custom_call_target="tpu_custom_call" | custom-call | tf_op jit(solution)/shard_map/pallas_call | solution.py:476
  108.8 0.0 copy-start
  108.8 3.3 %copy.14 = bf16[512,2048]{1,0:T(8,128)(2,1)} copy(bf16[512,2048]{1,0:T(8,128)(2,1)} %get-tuple-element.20) | data formatting | bytes 4194304
  112.1 0.0 copy-done
  112.1 0.0 copy-start.1
  112.1 0.0 copy-start.3
  112.1 0.0 copy-start.2
  112.1 2.0 %copy.15 = bf16[512,4096]{1,0:T(8,128)(2,1)} copy(bf16[512,4096]{1,0:T(8,128)(2,1)S(1)} %copy-done) | data formatting | bytes 8388608
  114.1 0.0 copy-done.1
  114.1 0.8 copy.16
  114.9 0.0 copy-done.3
  114.9 0.5 copy.17
  115.4 0.0 copy-done.2
  115.4 0.6 copy.18
Async XLA Ops:
  108.8 3.3 %copy-start = (bf16[512,4096]{1,0:T(8,128)(2,1)S(1)}, bf16[512,4096]{1,0:T(8,128)(2,1)}, u32[]{:S(2)}) copy-start(bf16[512,4096]{1,0:T(8,128)(2,1)} %get-tuple-element.21) | copy-start | bytes 12582916
  112.1 2.0 %copy-start.1 = (bf16[128,2048]{1,0:T(8,128)(2,1)S(1)}, bf16[128,2048]{1,0:T(8,128)(2,1)}, u32[]{:S(2)}) copy-start(bf16[128,2048]{1,0:T(8,128)(2,1)} %get-tuple-element.22) | copy-start | bytes 1572868
  112.1 2.8 %copy-start.3 = (f32[1,128]{1,0:T(1,128)S(1)}, f32[1,128]{1,0:T(1,128)}, u32[]{:S(2)}) copy-start(f32[1,128]{1,0:T(1,128)} %get-tuple-element.13) | copy-start | bytes 1540
  112.1 3.3 %copy-start.2 = (f32[1,2048]{1,0:T(1,128)S(1)}, f32[1,2048]{1,0:T(1,128)}, u32[]{:S(2)}) copy-start(f32[1,2048]{1,0:T(1,128)} %get-tuple-element.14) | copy-start | bytes 24580

commit v2 on v0

v2 whole, which is shorter than its diff:
```python
import jax
import jax.numpy as jnp
from jax import lax
from jax.experimental import pallas as pl
from jax.experimental.pallas import tpu as pltpu
from jax.sharding import Mesh
from jax.sharding import PartitionSpec as P

MESH = pl.DeviceIdType.MESH
BF, F32 = jnp.bfloat16, jnp.float32
EPS = 1e-06
ENTRIES = 4096 * 2048
OFFSET = (0, 1, 3, 2)
MORE = 32
ROWS = (128 + MORE, 128 - MORE)
PIECES = (
    ((0, 0, 128, 0), (128, 0, MORE, 1)),
    ((0, 0, 128, 2), (128, MORE, MORE, 1)),
    ((0, 0, 64, 3), (64, 2 * MORE, 64 - MORE, 1)),
    ((0, 64, 64, 3), (64, 64 + MORE, 64 - MORE, 1)),
)
PIECES = tuple(tuple(piece for piece in pieces if piece[2]) for pieces in PIECES)

FSDP = ("fx", "fy", "fc")
FSDP_DP = ("fx", "fy", "fc", "dp")
SIZE = {"fx": 4, "fy": 4, "fc": 2, "dp": 4}
ORDER = (("dp", "fx", "fy"), ("dp", "fy", "fx"), ("fx", "fy", "dp"), ("fy", "fx", "dp"))


def kernel(
    tok, cot, w, lv, ACC, IG, UP, ln_ref, rn_ref, inv_ref,
    W, T, TP, C, CP, Da, Db, R1a, R1b, R2a, R2b, Ea, Eb, Q1a, Q1b, Q2a, Q2b, Fa, Fb, R3a, R3b, GA,
    prc, prp, sqc, sqp, nmc, nmp, scal,
    ag_s, ag_r, fw_s, fw_r, ex_s, ex_r, rs_s, rs_r, p3_s, p3_r, gz_s, gz_r,
    c2_s, c2_r, pr_s, pr_r, sq_s, sq_r, nc_s, nc_r, np_s, np_r, ld_w, ld_c, ld_t,
):
    def colours(a, b):
        return [a.at[0], a.at[1], b.at[0], b.at[1]]

    D, R1, R2, E, Q1, Q2, F, R3 = (
        colours(a, b)
        for a, b in (
            (Da, Db), (R1a, R1b), (R2a, R2b), (Ea, Eb), (Q1a, Q1b), (Q2a, Q2b), (Fa, Fb), (R3a, R3b)
        )
    )
    pos = {name: lax.axis_index(name) for name in SIZE}
    mx, my, mc, mz = (pos[name] for name in ("fx", "fy", "fc", "dp"))
    oc = 1 - mc
    m1 = mx + mc * (my - mx)
    m2 = my + mc * (mx - my)

    def peer(name, step):
        return {name: (pos[name] + step) % SIZE[name]}

    def along1(step):
        return {"fx": (mx + oc * step) % 4, "fy": (my + mc * step) % 4}

    def along2(step):
        return {"fx": (mx + mc * step) % 4, "fy": (my + oc * step) % 4}

    def copy_to(src, dst, s, r, dev):
        return pltpu.make_async_remote_copy(
            src_ref=src, dst_ref=dst, send_sem=s, recv_sem=r, device_id=dev, device_id_type=MESH
        )

    def arrived(dst, sem):
        pltpu.make_async_copy(dst, dst, sem).wait()

    top, bottom, whole = pl.ds(0, 64), pl.ds(64, 64), pl.ds(0, 128)
    gather, landed = {}, {}
    for op in range(5):
        if op == 0:
            at = lambda step, rows=whole: W.at[mc, (m1 + step) % 4, m2, rows]
            dev = along1
        else:
            col = (m1 + OFFSET[op - 1]) % 4
            at = lambda step, rows=whole, col=col: W.at[mc, col, (m2 + step) % 4, rows]
            dev = along2
        src = (at(0), at(0), at(3, top), at(1, bottom))
        got = (at(3), at(1), at(2, top), at(2, bottom))
        for e, step in enumerate((1, 3, 1, 3)):
            gather[op, e] = copy_to(src[e], src[e], ag_s.at[op, e], ag_r.at[op, e], dev(step))
            landed[op, e] = (got[e], ag_r.at[op, e])
    partner = peer("fc", 1)
    across, crossed = [], []
    for slot in range(4):
        mine = W.at[mc, (m1 + OFFSET[slot]) % 4]
        across.append(copy_to(mine, mine, fw_s.at[slot], fw_r.at[slot], partner))
        crossed.append((W.at[oc, (m2 + OFFSET[slot]) % 4], fw_r.at[slot]))
    quarters = [pl.ds(pl.multiple_of(((mz + 6 - turn) % 4) * 512, 512), 512) for turn in range(4)]
    give_c = [
        copy_to(C.at[:, cs], CP.at[:, cs], ex_s.at[4 + i], ex_r.at[4 + i], partner)
        for i, cs in enumerate(quarters)
    ]
    give_t = [
        copy_to(T.at[oc, :, pl.ds(512 * g, 512)], TP.at[:, pl.ds(512 * g, 512)], ex_s.at[g], ex_r.at[g], partner)
        for g in range(4)
    ]

    ring = {}
    for ph, (S, A1, A2) in enumerate(((D, R1, R2), (E, Q1, Q2))):
        for k in range(4):
            name = ORDER[k][ph]
            m = pos[name]
            tp, tm, to = (m + 1) % 4, (m + 3) % 4, (m + 2) % 4
            plus, minus = peer(name, 1), peer(name, 3)
            a, b = pl.ds(0, 2), pl.ds(2, 2)
            moves = (
                (S[k].at[to, a], A1[k].at[0], plus),
                (S[k].at[to, b], A1[k].at[1], minus),
                (S[k].at[tp, b], A2[k].at[0, b], plus),
                (S[k].at[tm, a], A2[k].at[1, a], minus),
                (S[k].at[tp, a], A2[k].at[0, a], plus),
                (S[k].at[tm, b], A2[k].at[1, b], minus),
            )
            for e, (src, dst, dev) in enumerate(moves):
                ring[ph, k, e] = copy_to(src, dst, rs_s.at[ph, k, e], rs_r.at[ph, k, e], dev)
            ring[ph, k, "at"] = (m, tp, tm)
    last = {}
    for k in range(4):
        name = ORDER[k][2]
        for j in range(1, 4):
            to = (pos[name] + j) % 4
            last[k, j] = copy_to(F[k].at[to], R3[k].at[j - 1], p3_s.at[k, j - 1], p3_r.at[k, j - 1], {name: to})
    share = [
        copy_to(GA.at[mz], GA.at[mz], gz_s.at[j - 1], gz_r.at[j - 1], peer("dp", j)) for j in range(1, 4)
    ]

    def exchange(buf, s, r, slot_of, devices):
        here = slot_of(0)
        return [
            (copy_to(buf.at[here], buf.at[here], s.at[j], r.at[j], dev), buf.at[slot_of(j + 1)], r.at[j])
            for j, dev in enumerate(devices)
        ]

    plane_steps = [(i // 4, i % 4) for i in range(1, 16)]
    plane = [{"fx": (mx + i) % 4, "fy": (my + j) % 4} for i, j in plane_steps]
    cz_steps = [(i // 4, i % 4) for i in range(1, 8)]
    core_z = [{"fc": (mc + i) % 2, "dp": (mz + j) % 4} for i, j in cz_steps]

    def plane_slot(j):
        return ((mx + 4 - j // 4) % 4) * 4 + (my + 4 - j % 4) % 4

    def cz_slot(j):
        return ((mc + 2 - j // 4) % 2) * 4 + (mz + 4 - j % 4) % 4

    def core_slot(j):
        return (mc + j) % 2

    pr0 = exchange(prc, c2_s.at[pl.ds(0, 1)], c2_r.at[pl.ds(0, 1)], core_slot, [partner])
    pr1 = exchange(prp, pr_s, pr_r, plane_slot, plane)
    sq0 = exchange(sqc, c2_s.at[pl.ds(1, 1)], c2_r.at[pl.ds(1, 1)], core_slot, [partner])
    sq1 = exchange(sqp, sq_s, sq_r, plane_slot, plane)
    nm0 = exchange(nmc, nc_s, nc_r, cz_slot, core_z)
    nm1 = exchange(nmp, np_s, np_r, plane_slot, plane)

    def put(copies, buf, slot, value):
        buf[slot] = value
        for copy, _, _ in copies:
            copy.start()

    def total(copies, buf):
        for _, dst, sem in copies:
            arrived(dst, sem)
        value = buf[0]
        for j in range(1, buf.shape[0]):
            value = value + buf[j]
        return value

    load_w = pltpu.make_async_copy(w, W.at[mc, m1, m2], ld_w)
    load_w.start()
    load_c = pltpu.make_async_copy(cot, C, ld_c)
    load_c.start()
    for p in range(2):
        side = (oc + p) % 2
        for b in range(16):
            xy = b + side * ((b % 4) * 4 + b // 4 - b)
            pltpu.make_async_copy(
                tok.at[:, pl.ds(pl.multiple_of((2 * xy + side) * 128, 128), 128)],
                T.at[side, :, pl.ds(128 * b, 128)],
                ld_t.at[p, b // 4],
            ).start()

    def loaded(p, g):
        side = (oc + p) % 2
        region = T.at[side, :, pl.ds(512 * g, 512)]
        pltpu.make_async_copy(region, region, ld_t.at[p, g]).wait()

    barrier = pltpu.get_barrier_semaphore()
    others = plane + core_z
    for dev in others:
        pl.semaphore_signal(barrier, inc=1, device_id=dev, device_id_type=MESH)
    load_w.wait()
    w_wide = W[mc, m1, m2].astype(F32)
    lv_col = jnp.broadcast_to(lv[...], (128, 128)).T[:, 0:1]
    part_right = jnp.sum(w_wide * lv_col, axis=0, keepdims=True)
    prc[mc] = part_right
    ACC[...] = jnp.zeros((512, 2048), F32)
    pl.semaphore_wait(barrier, len(others))

    def spread(op):
        gather[op, 0].start()
        gather[op, 1].start()

    def forward(op):
        arrived(*landed[op, 0])
        gather[op, 2].start()
        arrived(*landed[op, 1])
        gather[op, 3].start()

    def cross(slot):
        arrived(*landed[slot + 1, 2])
        arrived(*landed[slot + 1, 3])
        across[slot].start()

    def meet():
        arrived(*landed[0, 2])
        arrived(*landed[0, 3])

    for copy, _, _ in pr0:
        copy.start()
    spread(0)
    load_c.wait()
    give_c[0].start()
    for g in range(4):
        loaded(0, g)
        give_t[g].start()
    for copy in give_c[1:]:
        copy.start()
    put(pr1, prp, mx * 4 + my, total(pr0, prc))
    spread(1)

    def ring_go(ph, k, *events):
        for e in events:
            ring[ph, k, e].start()

    def ring_mid(ph, k):
        S, A1 = ((D, R1), (E, Q1))[ph]
        _, tp, tm = ring[ph, k, "at"]
        for d, (t, lo_, e) in enumerate(((tp, 0, 4), (tm, 2, 5))):
            arrived(A1[k].at[d], rs_r.at[ph, k, d])
            for i in range(2):
                S[k][t, lo_ + i] = (S[k][t, lo_ + i].astype(F32) + A1[k][d, i].astype(F32)).astype(BF)
            ring[ph, k, e].start()

    def ring_end(ph, k):
        S, A2, out = ((D, R2, E), (E, Q2, F))[ph]
        m = ring[ph, k, "at"][0]
        a, b = pl.ds(0, 2), pl.ds(2, 2)
        arrived(A2[k].at[0, b], rs_r.at[ph, k, 2])
        arrived(A2[k].at[1, a], rs_r.at[ph, k, 3])
        arrived(A2[k].at[0, a], rs_r.at[ph, k, 4])
        arrived(A2[k].at[1, b], rs_r.at[ph, k, 5])
        for i in range(4):
            out[k][i] = (
                S[k][m, i].astype(F32) + A2[k][0, i].astype(F32) + A2[k][1, i].astype(F32)
            ).astype(BF)

    def p1_end(k):
        ring_end(0, k)
        ring_go(1, k, 0, 1, 2, 3)

    def p2_end(k):
        ring_end(1, k)
        for j in range(1, 4):
            last[k, j].start()

    def sq_start():
        right_raw = total(pr1, prp)
        right_next = right_raw / jnp.sqrt(jnp.sum(right_raw * right_raw) + EPS)
        rn_ref[...] = right_next
        left_raw = jnp.sum(W[mc, m1, m2].astype(F32) * right_next, axis=1, keepdims=True)
        put(sq0, sqc, mc, jnp.broadcast_to(jnp.sum(left_raw * left_raw, keepdims=True), (8, 128)))

    def sq_plane():
        put(sq1, sqp, mx * 4 + my, total(sq0, sqc))

    def sq_end():
        left_sq = total(sq1, sqp)
        scal[0] = left_sq
        inv_ref[...] = 1.0 / jnp.sqrt(left_sq + EPS)

    def wait_c(turn):
        arrived(CP.at[:, quarters[turn]], ex_r.at[4 + turn])

    def wait_t(g):
        arrived(TP.at[:, pl.ds(512 * g, 512)], ex_r.at[g])
        loaded(1, g)

    wait_c(0)
    over_tokens = (((0,), (0,)), ((), ()))

    def run(events, i):
        for when, todo in events.items():
            @pl.when(i == when)
            def _():
                for f, *a in todo:
                    f(*a)

    def term(i, carry):
        turn = i // 4
        g = i % 4
        run(TERM_WAITS, i)
        q = (mz + 6 - turn) % 4
        cs = pl.ds(pl.multiple_of(q * 512, 512), 512)
        ms = pl.ds(pl.multiple_of(g * 512, 512), 512)
        r = lax.dot_general(T[mc, :, ms], C[:, cs], over_tokens, preferred_element_type=F32)
        r = r + lax.dot_general(TP[:, ms], CP[:, cs], over_tokens, preferred_element_type=F32)
        r = r.astype(BF)
        for h in range(4):
            x = g + mc * (h - g)
            y = h + mc * (g - h)
            at = ((q, x, y), (q, y, x), (x, y, q), (y, x, q))
            for k in range(4):
                for u, b, n, tile in PIECES[k]:
                    rows = slice(128 * h + b, 128 * h + b + n)
                    D[k][(*at[k], slice(u, u + n))] = r[rows, 128 * tile : 128 * tile + 128]
        run(TERM_EVENTS, i)
        return carry

    TERM_WAITS = {
        0: [(wait_t, 0)],
        1: [(wait_t, 1)],
        2: [(wait_t, 2)],
        3: [(wait_t, 3)],
        4: [(wait_c, 1)],
        8: [(wait_c, 2)],
        12: [(wait_c, 3)],
    }
    TERM_EVENTS = {
        3: [(ring_go, 0, 0, 0, 1), (ring_go, 0, 1, 0, 1)],
        7: [(ring_go, 0, 0, 2), (ring_go, 0, 1, 2)],
        10: [(forward, 1), (forward, 0), (spread, 2)],
        12: [(sq_start,)],
        14: [(sq_plane,)],
        15: [
            (ring_go, 0, 2, 0, 1, 2, 3), (ring_go, 0, 3, 0, 1, 2, 3),
            (ring_go, 0, 0, 3), (ring_go, 0, 1, 3),
        ],
    }
    lax.fori_loop(0, 16, term, 0)

    def group(slot):
        arrived(*crossed[slot])

    def norms():
        inv = inv_ref[0:1, 0:1]
        quarter = pl.ds(pl.multiple_of(mz * 512, 512), 512)
        rn = rn_ref[:, quarter]
        wq = W[mc, m1, m2, :, quarter].astype(F32)
        raw = jnp.sum(W[mc, m1, m2].astype(F32) * rn_ref[...], axis=1, keepdims=True)
        ln = raw * inv
        sums = [jnp.zeros((1, 128), F32)] * 3
        for k in range(4):
            unit = F[k][pos[ORDER[k][2]]].astype(F32)
            for j in range(3):
                arrived(R3[k].at[j], p3_r.at[k, j])
                unit = unit + R3[k][j].astype(F32)
            for u, b, n, tile in PIECES[k]:
                g, rows, cols = unit[u : u + n], slice(b, b + n), slice(128 * tile, 128 * tile + 128)
                GA[mz, rows, cols] = g.astype(BF)
                sums[0] = sums[0] + jnp.sum(g * g, axis=0, keepdims=True)
                sums[1] = sums[1] + jnp.sum(g * wq[rows, cols], axis=0, keepdims=True)
                sums[2] = sums[2] + jnp.sum(g * ln[rows], axis=0, keepdims=True) * rn[:, cols]
        put(nm0, nmc, mc * 4 + mz, jnp.concatenate(sums + [jnp.zeros((5, 128), F32)], axis=0))
        for copy in share:
            copy.start()

    def nm_plane():
        put(nm1, nmp, mx * 4 + my, total(nm0, nmc))

    def both(s, carry):
        run(BOTH_EVENTS, s)
        early = s < 4
        kind = jnp.where(early, s // 2, s % 2)
        i = jnp.where(early, s % 2, s // 2)
        slot, other = i // 2, i % 2
        off = slot + slot // 2 - 2 * (slot // 3)
        p = (mc + other) % 2
        col = (m1 + other * (m2 - m1) + off) % 4

        @pl.when(kind == 0)
        def _():
            ms = pl.ds(pl.multiple_of(col * 512, 512), 512)
            for n in range(4):
                cs = slice(512 * n, 512 * n + 512)
                rows = W[p, col, :, :, cs].reshape(512, 512)
                ACC[:, cs] = ACC[:, cs] + jnp.dot(T[p, :, ms], rows, preferred_element_type=F32)

        @pl.when(kind == 1)
        def _():
            inv = inv_ref[0:1, 0:1]
            rows = W[p, col].reshape(512, 2048)
            r = lax.dot_general(C[...], rows, (((1,), (1,)), ((), ())), preferred_element_type=F32)
            r = (r * inv).astype(BF)
            for h in range(4):
                x = col + p * (h - col)
                y = h + p * (col - h)
                at = pl.multiple_of(((x * 4 + y) * 2 + p) * 128, 128)
                IG[:, pl.ds(at, 128)] = r[:, 128 * h : 128 * h + 128]

        return carry

    BOTH_EVENTS = {
        0: [(cross, 0)],
        1: [(ring_mid, 0, 0), (ring_mid, 0, 1), (group, 0)],
        2: [(sq_end,)],
        4: [(forward, 2), (ring_mid, 0, 2), (ring_mid, 0, 3), (spread, 3), (meet,), (cross, 1)],
        5: [(p1_end, 2), (p1_end, 3)],
        6: [(group, 1)],
        8: [
            (forward, 3), (p1_end, 0), (p1_end, 1), (spread, 4),
            (ring_mid, 1, 2), (ring_mid, 1, 3), (cross, 2),
        ],
        9: [(ring_mid, 1, 0), (ring_mid, 1, 1)],
        10: [(p2_end, 2), (p2_end, 3), (group, 2)],
        11: [(p2_end, 0), (p2_end, 1)],
        12: [(forward, 4), (norms,), (cross, 3)],
        13: [(nm_plane,)],
        14: [(group, 3)],
    }
    lax.fori_loop(0, 16, both, 0)

    inv = inv_ref[0:1, 0:1]
    sums = jnp.sum(total(nm1, nmp), axis=1, keepdims=True)
    grad_sq_raw, inner, crossed_term = sums[0:1], sums[1:2], sums[2:3]
    lsq = scal[0][0:1, 0:1]
    sq = lsq + EPS
    coeff = inner / sq
    rn = rn_ref[...]
    raw = jnp.sum(W[mc, m1, m2].astype(F32) * rn, axis=1, keepdims=True)
    ln = raw * inv
    ln_ref[...] = jnp.broadcast_to(ln, (128, 128)).T[0:1]
    right_unit = jnp.sum(rn * rn, keepdims=True)
    grad_sq = (
        grad_sq_raw / sq - 2.0 * coeff * crossed_term * inv + coeff * coeff * (lsq / sq) * right_unit
    )
    inv_rms = 1.0 / jnp.sqrt(grad_sq / ENTRIES + EPS)
    for j in range(1, 4):
        arrived(GA.at[(mz + 4 - j) % 4], gz_r.at[j - 1])
    scale = inv * inv_rms
    column = ln * (coeff * inv_rms)
    for q in range(4):
        cs = slice(512 * q, 512 * q + 512)
        UP[:, cs] = (GA[q].astype(F32) * scale - column * rn[:, cs]).astype(BF)

    for copy in list(gather.values()) + across + give_c + give_t + list(last.values()) + share:
        copy.wait_send()
    for key, copy in ring.items():
        if key[2] != "at":
            copy.wait_send()
    for copies in (pr0, pr1, sq0, sq1, nm0, nm1):
        for copy, _, _ in copies:
            copy.wait_send()


def write_out(acc, ig, up, ln, rn, inv, lo_out, ig_out, up_out, ln_out, rn_out, lo, sems):
    copies = [
        pltpu.make_async_copy(src, dst, sems.at[i])
        for i, (src, dst) in enumerate(((ig, ig_out), (up, up_out), (ln, ln_out), (rn, rn_out)))
    ]
    for copy in copies:
        copy.start()
    for n in range(4):
        rows = pl.ds(128 * n, 128)
        lo[rows] = (acc[rows] * inv[0:1, 0:1]).astype(BF)
        copy = pltpu.make_async_copy(lo.at[rows], lo_out.at[rows], sems.at[4 + n])
        copy.start()
        copies.append(copy)
    for copy in copies:
        copy.wait()


def per_device(tokens, cotangent, weight, left_vector):
    dma = pltpu.SemaphoreType.DMA
    vm = pltpu.VMEM
    hbm = pl.BlockSpec(memory_space=pl.ANY)
    vmem = pl.BlockSpec(memory_space=pltpu.VMEM)
    outs = pl.pallas_call(
        kernel,
        out_shape=(
            vm((512, 2048), F32),
            vm((512, 4096), BF),
            vm((128, 2048), BF),
            vm((1, 128), F32),
            vm((1, 2048), F32),
            vm((8, 128), F32),
        ),
        in_specs=[hbm, hbm, hbm, vmem],
        out_specs=(vmem,) * 6,
        scratch_shapes=[
            vm((2, 4, 4, 128, 2048), BF),
            vm((2, 512, 2048), BF),
            vm((512, 2048), BF),
            vm((512, 2048), BF),
            vm((512, 2048), BF),
            *[
                vm((2, *dims, rows, 128), BF)
                for dims in ((4, 4, 4), (2, 2, 4), (2, 4, 4), (4, 4), (2, 2), (2, 4), (4,), (3,))
                for rows in ROWS
            ],
            vm((4, 128, 512), BF),
            vm((2, 1, 2048), F32),
            vm((16, 1, 2048), F32),
            vm((2, 8, 128), F32),
            vm((16, 8, 128), F32),
            vm((8, 8, 128), F32),
            vm((16, 8, 128), F32),
            vm((1, 8, 128), F32),
            dma((5, 4)),
            dma((5, 4)),
            dma((4,)),
            dma((4,)),
            dma((8,)),
            dma((8,)),
            dma((2, 4, 6)),
            dma((2, 4, 6)),
            dma((4, 3)),
            dma((4, 3)),
            dma((3,)),
            dma((3,)),
            dma((2,)),
            dma((2,)),
            dma((15,)),
            dma((15,)),
            dma((15,)),
            dma((15,)),
            dma((7,)),
            dma((7,)),
            dma((15,)),
            dma((15,)),
            dma,
            dma,
            dma((2, 4)),
        ],
        compiler_params=pltpu.CompilerParams(
            collective_id=0, has_side_effects=True, vmem_limit_bytes=50 * 2**20
        ),
    )(tokens, cotangent, weight, left_vector.reshape(1, 128))
    layer_out, input_grad, update, left_next, right_next = pl.pallas_call(
        write_out,
        out_shape=(
            jax.ShapeDtypeStruct((512, 2048), BF),
            jax.ShapeDtypeStruct((512, 4096), BF),
            jax.ShapeDtypeStruct((128, 2048), BF),
            jax.ShapeDtypeStruct((1, 128), F32),
            jax.ShapeDtypeStruct((1, 2048), F32),
        ),
        in_specs=[vmem] * 6,
        out_specs=(hbm,) * 5,
        scratch_shapes=[vm((512, 2048), BF), dma((8,))],
        compiler_params=pltpu.CompilerParams(vmem_limit_bytes=6 * 2**20),
    )(*[pltpu.with_memory_space_constraint(o, pltpu.VMEM) for o in outs])
    return (layer_out, input_grad, update, left_next.reshape(128), right_next.reshape(2048))


def solution(mesh):
    torus = Mesh(mesh.devices.reshape(4, 4, 2, mesh.shape["dp"]), FSDP_DP)
    return jax.shard_map(
        per_device,
        mesh=torus,
        in_specs=(P(FSDP_DP, None), P(FSDP_DP, None), P(FSDP, None), P(FSDP)),
        out_specs=(P(FSDP_DP, None), P(FSDP_DP, None), P(FSDP, None), P(FSDP), P()),
        check_vma=False,
    )
```

time: 248 us -> 101 us (0.41)
  waiting for transfers between devices: 116 us -> 0 us
  Pallas kernels: 0 us -> 101 us
  matrix products: 40.3 us -> 0 us
  blocking collectives: 28.8 us -> 0 us
  local copies, waits for them, and re-layouts: 20.4 us -> 0 us
  between operations: 20.2 us -> 0.64 us
  starting transfers between devices: 12.6 us -> 0 us
  other arithmetic: 9.01 us -> 0 us
    pallas_call x0 -> x2, Pallas kernels: none -> 101 us  [the longest x1 97.8 us: per_device(): pl.pallas_call(kernel, out_shape=(vm((512, 2048), F32), vm((512, 4096), B...]
    all_gather x2 -> x0, waiting for transfers between devices: 60.4 us -> none  [gather_in_order(): blocks = lax.all_gather(blocks, axes[k], axis=0, tiled=True)]
    dot_general x6 -> x0, matrix products: 40.3 us -> none  [the longest x1 14.6 us: per_device(): lax.dot_general(tokens, cotangent, (((0,), (0,)), ((), ())), preferred_el...]
    all_to_all x2 -> x0, waiting for transfers between devices: 29.3 us -> none  [sent_to_all(): return lax.all_to_all(copies, axis, split_axis=0, concat_axis=0, tiled=True)]
    all_to_all x2 -> x0, blocking collectives: 28.8 us -> none  [sent_to_all(): return lax.all_to_all(copies, axis, split_axis=0, concat_axis=0, tiled=True)]
    reduce_scatter x1 -> x0, waiting for transfers between devices: 26 us -> none  [per_device(): lax.psum_scatter(lax.dot_general(tokens, cotangent, (((0,), (0,)), ((), (...]
    all_to_all x2 -> x0, starting transfers between devices: 12.5 us -> none  [sent_to_all(): return lax.all_to_all(copies, axis, split_axis=0, concat_axis=0, tiled=True)]
    transpose x1 -> x0, local copies, waits for them, and re-layouts: 8.26 us -> none  [gather_in_order(): blocks.transpose(*turned, *range(len(order), blocks.ndim))]
  transfers between devices with their start and end apart: 5 -> 0, of which waited for: 4 -> 0; matrix products, arithmetic and copies ran while one was open for 12% -> 0% of each run, Pallas kernels for 0% -> 0%
where the time goes in v2:
time: 101 us
  Pallas kernels  101 us (100%)
    pallas_call x1, Pallas kernels, per_device(): pl.pallas_call(kernel, out_shape=(vm((512, 2048), F32), vm((512, 4096), B...  97.8 us
    pallas_call x1, Pallas kernels, per_device(): pl.pallas_call(write_out, out_shape=(jax.ShapeDtypeStruct((512, 2048), BF...  2.88 us

profile of v2, /device:TPU:1, one launch (start us, length us, event | category | flops | bytes accessed | tf_op | source)
XLA Modules:
  0.0 101.3 jit_solution(4819737483083159339)
XLA Ops:
  0.6 97.8 %shard_map.83 = (f32[512,2048]{1,0:T(8,128)S(1)}, bf16[512,4096]{1,0:T(8,128)(2,1)S(1)}, bf16[128,2048]{1,0:T(8,128)(2,1)S(1)}, f32[1,128]{1,0:T(1,128)S(1)}, f3...) custom-call(bf16[512,4096]{1,0:T(8,128)(2,1)} %tok.1, bf16[512,2048]{1,0:T(8,128)(2,1)} %cot.1, bf16[128,2048]{1,0:T(8,128)(2,1)} %w.1, ...), custom_call_target="tpu_custom_call" | custom-call | tf_op jit(solution)/shard_map/pallas_call | solution.py:479
  98.4 2.9 %shard_map.84 = (bf16[512,2048]{1,0:T(8,128)(2,1)}, bf16[512,4096]{1,0:T(8,128)(2,1)}, bf16[128,2048]{1,0:T(8,128)(2,1)}, f32[1,128]{1,0:T(1,128)}, f32[1,2048]{1,0:T(1,128)}) custom-call(f32[512,2048]{1,0:T(8,128)S(1)} %get-tuple-element.16.acc, bf16[512,4096]{1,0:T(8,128)(2,1)S(1)} %get-tuple-element.17.ig, bf16[128,2048]{1,0:T(8,128)(2,1)S(1)} %get-tuple-element.18.up, ...), custom_call_target="tpu_custom_call" | custom-call | tf_op jit(solution)/shard_map/pallas_call | solution.py:540

commit v3 on v2

--- a/solution.py
+++ b/solution.py
@@ -32,7 +32,7 @@
     W, T, TP, C, CP, Da, Db, R1a, R1b, R2a, R2b, Ea, Eb, Q1a, Q1b, Q2a, Q2b, Fa, Fb, R3a, R3b, GA,
     prc, prp, sqc, sqp, nmc, nmp, scal,
     ag_s, ag_r, fw_s, fw_r, ex_s, ex_r, rs_s, rs_r, p3_s, p3_r, gz_s, gz_r,
-    c2_s, c2_r, pr_s, pr_r, sq_s, sq_r, nc_s, nc_r, np_s, np_r, ld_w, ld_c, ld_t,
+    sm_s, sm_r, ld_w, ld_c, ld_t,
 ):
     def colours(a, b):
         return [a.at[0], a.at[1], b.at[0], b.at[1]]
@@ -77,23 +77,28 @@
             at = lambda step, rows=whole, col=col: W.at[mc, col, (m2 + step) % 4, rows]
             dev = along2
         src = (at(0), at(0), at(3, top), at(1, bottom))
-        got = (at(3), at(1), at(2, top), at(2, bottom))
+        got = (at(3), at(1))
         for e, step in enumerate((1, 3, 1, 3)):
-            gather[op, e] = copy_to(src[e], src[e], ag_s.at[op, e], ag_r.at[op, e], dev(step))
-            landed[op, e] = (got[e], ag_r.at[op, e])
+            gather[op, e] = copy_to(src[e], src[e], ag_s.at[min(op, 1)], ag_r.at[op, min(e, 2)], dev(step))
+        landed[op, 0], landed[op, 1] = (got[0], ag_r.at[op, 0]), (got[1], ag_r.at[op, 1])
+        landed[op, 2] = (at(2), ag_r.at[op, 2])
     partner = peer("fc", 1)
     across, crossed = [], []
-    for slot in range(4):
+    for slot in range(3):
         mine = W.at[mc, (m1 + OFFSET[slot]) % 4]
-        across.append(copy_to(mine, mine, fw_s.at[slot], fw_r.at[slot], partner))
+        across.append(copy_to(mine, mine, fw_s.at[0], fw_r.at[slot], partner))
         crossed.append((W.at[oc, (m2 + OFFSET[slot]) % 4], fw_r.at[slot]))
+    for step, at in enumerate(OFFSET):
+        mine = W.at[mc, (m1 + 2) % 4, (m2 + at) % 4]
+        across.append(copy_to(mine, mine, fw_s.at[0], fw_r.at[3 + step], partner))
+        crossed.append((W.at[oc, (m2 + 2) % 4, (m1 + at) % 4], fw_r.at[3 + step]))
     quarters = [pl.ds(pl.multiple_of(((mz + 6 - turn) % 4) * 512, 512), 512) for turn in range(4)]
     give_c = [
-        copy_to(C.at[:, cs], CP.at[:, cs], ex_s.at[4 + i], ex_r.at[4 + i], partner)
+        copy_to(C.at[:, cs], CP.at[:, cs], ex_s.at[0], ex_r.at[4 + i], partner)
         for i, cs in enumerate(quarters)
     ]
     give_t = [
-        copy_to(T.at[oc, :, pl.ds(512 * g, 512)], TP.at[:, pl.ds(512 * g, 512)], ex_s.at[g], ex_r.at[g], partner)
+        copy_to(T.at[oc, :, pl.ds(512 * g, 512)], TP.at[:, pl.ds(512 * g, 512)], ex_s.at[0], ex_r.at[g], partner)
         for g in range(4)
     ]
 
@@ -114,54 +119,41 @@
                 (S[k].at[tm, b], A2[k].at[1, b], minus),
             )
             for e, (src, dst, dev) in enumerate(moves):
-                ring[ph, k, e] = copy_to(src, dst, rs_s.at[ph, k, e], rs_r.at[ph, k, e], dev)
+                ring[ph, k, e] = copy_to(src, dst, rs_s.at[ph, k], rs_r.at[ph, k, min(e, 2)], dev)
             ring[ph, k, "at"] = (m, tp, tm)
     last = {}
     for k in range(4):
         name = ORDER[k][2]
         for j in range(1, 4):
             to = (pos[name] + j) % 4
-            last[k, j] = copy_to(F[k].at[to], R3[k].at[j - 1], p3_s.at[k, j - 1], p3_r.at[k, j - 1], {name: to})
+            last[k, j] = copy_to(F[k].at[to], R3[k].at[j - 1], p3_s.at[k], p3_r.at[k], {name: to})
     share = [
-        copy_to(GA.at[mz], GA.at[mz], gz_s.at[j - 1], gz_r.at[j - 1], peer("dp", j)) for j in range(1, 4)
+        copy_to(GA.at[mz], GA.at[mz], gz_s.at[0], gz_r.at[0], peer("dp", j)) for j in range(1, 4)
     ]
 
-    def exchange(buf, s, r, slot_of, devices):
-        here = slot_of(0)
-        return [
-            (copy_to(buf.at[here], buf.at[here], s.at[j], r.at[j], dev), buf.at[slot_of(j + 1)], r.at[j])
-            for j, dev in enumerate(devices)
-        ]
+    def exchange(buf, s, r, here, devices):
+        return [copy_to(buf.at[here], buf.at[here], s, r, dev) for dev in devices], r
 
     plane_steps = [(i // 4, i % 4) for i in range(1, 16)]
     plane = [{"fx": (mx + i) % 4, "fy": (my + j) % 4} for i, j in plane_steps]
     cz_steps = [(i // 4, i % 4) for i in range(1, 8)]
     core_z = [{"fc": (mc + i) % 2, "dp": (mz + j) % 4} for i, j in cz_steps]
 
-    def plane_slot(j):
-        return ((mx + 4 - j // 4) % 4) * 4 + (my + 4 - j % 4) % 4
-
-    def cz_slot(j):
-        return ((mc + 2 - j // 4) % 2) * 4 + (mz + 4 - j % 4) % 4
-
-    def core_slot(j):
-        return (mc + j) % 2
-
-    pr0 = exchange(prc, c2_s.at[pl.ds(0, 1)], c2_r.at[pl.ds(0, 1)], core_slot, [partner])
-    pr1 = exchange(prp, pr_s, pr_r, plane_slot, plane)
-    sq0 = exchange(sqc, c2_s.at[pl.ds(1, 1)], c2_r.at[pl.ds(1, 1)], core_slot, [partner])
-    sq1 = exchange(sqp, sq_s, sq_r, plane_slot, plane)
-    nm0 = exchange(nmc, nc_s, nc_r, cz_slot, core_z)
-    nm1 = exchange(nmp, np_s, np_r, plane_slot, plane)
+    here = mx * 4 + my
+    pr0 = exchange(prc, sm_s.at[0], sm_r.at[0], mc, [partner])
+    pr1 = exchange(prp, sm_s.at[1], sm_r.at[1], here, plane)
+    sq0 = exchange(sqc, sm_s.at[2], sm_r.at[2], mc, [partner])
+    sq1 = exchange(sqp, sm_s.at[3], sm_r.at[3], here, plane)
+    nm0 = exchange(nmc, sm_s.at[4], sm_r.at[4], mc * 4 + mz, core_z)
+    nm1 = exchange(nmp, sm_s.at[5], sm_r.at[5], here, plane)
 
     def put(copies, buf, slot, value):
         buf[slot] = value
-        for copy, _, _ in copies:
+        for copy in copies[0]:
             copy.start()
 
     def total(copies, buf):
-        for _, dst, sem in copies:
-            arrived(dst, sem)
+        arrived(buf.at[pl.ds(0, buf.shape[0] - 1)], copies[1])
         value = buf[0]
         for j in range(1, buf.shape[0]):
             value = value + buf[j]
@@ -169,6 +161,17 @@
 
     load_w = pltpu.make_async_copy(w, W.at[mc, m1, m2], ld_w)
     load_w.start()
+    def loaded(p, g):
+        side = (oc + p) % 2
+        region = T.at[side, :, pl.ds(512 * g, 512)]
+        pltpu.make_async_copy(region, region, ld_t.at[p, g]).wait()
+
+    barrier = pltpu.get_barrier_semaphore()
+    others = plane + core_z
+    for dev in others:
+        pl.semaphore_signal(barrier, inc=1, device_id=dev, device_id_type=MESH)
+    ACC[...] = jnp.zeros((512, 2048), F32)
+    load_w.wait()
     load_c = pltpu.make_async_copy(cot, C, ld_c)
     load_c.start()
     for p in range(2):
@@ -181,21 +184,10 @@
                 ld_t.at[p, b // 4],
             ).start()
 
-    def loaded(p, g):
-        side = (oc + p) % 2
-        region = T.at[side, :, pl.ds(512 * g, 512)]
-        pltpu.make_async_copy(region, region, ld_t.at[p, g]).wait()
-
-    barrier = pltpu.get_barrier_semaphore()
-    others = plane + core_z
-    for dev in others:
-        pl.semaphore_signal(barrier, inc=1, device_id=dev, device_id_type=MESH)
-    load_w.wait()
     w_wide = W[mc, m1, m2].astype(F32)
     lv_col = jnp.broadcast_to(lv[...], (128, 128)).T[:, 0:1]
     part_right = jnp.sum(w_wide * lv_col, axis=0, keepdims=True)
     prc[mc] = part_right
-    ACC[...] = jnp.zeros((512, 2048), F32)
     pl.semaphore_wait(barrier, len(others))
 
     def spread(op):
@@ -210,16 +202,24 @@
 
     def cross(slot):
         arrived(*landed[slot + 1, 2])
-        arrived(*landed[slot + 1, 3])
         across[slot].start()
+
+    def cross_first():
+        for i in (3, 4, 5):
+            across[i].start()
+
+    def cross_last():
+        arrived(*landed[4, 2])
+        across[6].start()
 
     def meet():
         arrived(*landed[0, 2])
-        arrived(*landed[0, 3])
-
-    for copy, _, _ in pr0:
+
+    for copy in pr0[0]:
         copy.start()
+    put(pr1, prp, mx * 4 + my, total(pr0, prc))
     spread(0)
+    spread(1)
     load_c.wait()
     give_c[0].start()
     for g in range(4):
@@ -227,8 +227,6 @@
         give_t[g].start()
     for copy in give_c[1:]:
         copy.start()
-    put(pr1, prp, mx * 4 + my, total(pr0, prc))
-    spread(1)
 
     def ring_go(ph, k, *events):
         for e in events:
@@ -246,11 +244,7 @@
     def ring_end(ph, k):
         S, A2, out = ((D, R2, E), (E, Q2, F))[ph]
         m = ring[ph, k, "at"][0]
-        a, b = pl.ds(0, 2), pl.ds(2, 2)
-        arrived(A2[k].at[0, b], rs_r.at[ph, k, 2])
-        arrived(A2[k].at[1, a], rs_r.at[ph, k, 3])
-        arrived(A2[k].at[0, a], rs_r.at[ph, k, 4])
-        arrived(A2[k].at[1, b], rs_r.at[ph, k, 5])
+        arrived(A2[k], rs_r.at[ph, k, 2])
         for i in range(4):
             out[k][i] = (
                 S[k][m, i].astype(F32) + A2[k][0, i].astype(F32) + A2[k][1, i].astype(F32)
@@ -329,10 +323,10 @@
     }
     TERM_EVENTS = {
         3: [(ring_go, 0, 0, 0, 1), (ring_go, 0, 1, 0, 1)],
-        7: [(ring_go, 0, 0, 2), (ring_go, 0, 1, 2)],
-        10: [(forward, 1), (forward, 0), (spread, 2)],
-        12: [(sq_start,)],
-        14: [(sq_plane,)],
+        5: [(sq_start,)],
+        7: [(ring_go, 0, 0, 2), (ring_go, 0, 1, 2), (sq_plane,)],
+        11: [(forward, 1), (forward, 0), (spread, 2)],
+        14: [(sq_end,)],
         15: [
             (ring_go, 0, 2, 0, 1, 2, 3), (ring_go, 0, 3, 0, 1, 2, 3),
             (ring_go, 0, 0, 3), (ring_go, 0, 1, 3),
@@ -353,8 +347,8 @@
         sums = [jnp.zeros((1, 128), F32)] * 3
         for k in range(4):
             unit = F[k][pos[ORDER[k][2]]].astype(F32)
+            arrived(R3[k], p3_r.at[k])
             for j in range(3):
-                arrived(R3[k].at[j], p3_r.at[k, j])
                 unit = unit + R3[k][j].astype(F32)
             for u, b, n, tile in PIECES[k]:
                 g, rows, cols = unit[u : u + n], slice(b, b + n), slice(128 * tile, 128 * tile + 128)
@@ -371,9 +365,7 @@
 
     def both(s, carry):
         run(BOTH_EVENTS, s)
-        early = s < 4
-        kind = jnp.where(early, s // 2, s % 2)
-        i = jnp.where(early, s % 2, s // 2)
+        kind, i = s % 2, s // 2
         slot, other = i // 2, i % 2
         off = slot + slot // 2 - 2 * (slot // 3)
         p = (mc + other) % 2
@@ -403,23 +395,58 @@
 
     BOTH_EVENTS = {
         0: [(cross, 0)],
-        1: [(ring_mid, 0, 0), (ring_mid, 0, 1), (group, 0)],
-        2: [(sq_end,)],
+        2: [(group, 0)],
+        3: [(ring_mid, 0, 0), (ring_mid, 0, 1)],
         4: [(forward, 2), (ring_mid, 0, 2), (ring_mid, 0, 3), (spread, 3), (meet,), (cross, 1)],
-        5: [(p1_end, 2), (p1_end, 3)],
         6: [(group, 1)],
+        7: [(p1_end, 2), (p1_end, 3)],
         8: [
-            (forward, 3), (p1_end, 0), (p1_end, 1), (spread, 4),
-            (ring_mid, 1, 2), (ring_mid, 1, 3), (cross, 2),
+            (p1_end, 0), (p1_end, 1), (forward, 3),
+            (ring_mid, 1, 2), (ring_mid, 1, 3), (ring_mid, 1, 0), (ring_mid, 1, 1),
+            (spread, 4), (cross, 2),
         ],
-        9: [(ring_mid, 1, 0), (ring_mid, 1, 1)],
-        10: [(p2_end, 2), (p2_end, 3), (group, 2)],
-        11: [(p2_end, 0), (p2_end, 1)],
-        12: [(forward, 4), (norms,), (cross, 3)],
-        13: [(nm_plane,)],
-        14: [(group, 3)],
+        10: [(p2_end, 2), (p2_end, 3), (p2_end, 0), (p2_end, 1), (group, 2)],
     }
-    lax.fori_loop(0, 16, both, 0)
+    lax.fori_loop(0, 12, both, 0)
+
+    def halves(s, carry):
+        run(HALF_EVENTS, s)
+        kind, other, late = s % 2, (s // 2) % 2, s // 4
+        p = (mc + other) % 2
+        a1 = (m1 + other * (m2 - m1) + 2) % 4
+        base = m2 + other * (m1 - m2)
+        a2 = ((base + 3 * late) % 4, (base + 1 + late) % 4)
+
+        @pl.when(kind == 0)
+        def _():
+            cols = [T[p, :, pl.ds(pl.multiple_of((a1 * 4 + v) * 128, 128), 128)] for v in a2]
+            toks = jnp.concatenate(cols, axis=1)
+            for n in range(4):
+                cs = slice(512 * n, 512 * n + 512)
+                rows = jnp.concatenate([W[p, a1, v, :, cs] for v in a2], axis=0)
+                ACC[:, cs] = ACC[:, cs] + jnp.dot(toks, rows, preferred_element_type=F32)
+
+        @pl.when(kind == 1)
+        def _():
+            inv = inv_ref[0:1, 0:1]
+            rows = jnp.concatenate([W[p, a1, v] for v in a2], axis=0)
+            r = lax.dot_general(C[...], rows, (((1,), (1,)), ((), ())), preferred_element_type=F32)
+            r = (r * inv).astype(BF)
+            for h, v in enumerate(a2):
+                x = a1 + p * (v - a1)
+                y = v + p * (a1 - v)
+                at = pl.multiple_of(((x * 4 + y) * 2 + p) * 128, 128)
+                IG[:, pl.ds(at, 128)] = r[:, 128 * h : 128 * h + 128]
+
+        return carry
+
+    HALF_EVENTS = {
+        0: [(forward, 4), (cross_first,)],
+        2: [(norms,), (group, 3), (group, 4)],
+        4: [(nm_plane,), (cross_last,)],
+        6: [(group, 5), (group, 6)],
+    }
+    lax.fori_loop(0, 8, halves, 0)
 
     inv = inv_ref[0:1, 0:1]
     sums = jnp.sum(total(nm1, nmp), axis=1, keepdims=True)
@@ -436,22 +463,27 @@
         grad_sq_raw / sq - 2.0 * coeff * crossed_term * inv + coeff * coeff * (lsq / sq) * right_unit
     )
     inv_rms = 1.0 / jnp.sqrt(grad_sq / ENTRIES + EPS)
-    for j in range(1, 4):
-        arrived(GA.at[(mz + 4 - j) % 4], gz_r.at[j - 1])
+    arrived(GA.at[pl.ds(0, 3)], gz_r.at[0])
     scale = inv * inv_rms
     column = ln * (coeff * inv_rms)
     for q in range(4):
         cs = slice(512 * q, 512 * q + 512)
         UP[:, cs] = (GA[q].astype(F32) * scale - column * rn[:, cs]).astype(BF)
 
-    for copy in list(gather.values()) + across + give_c + give_t + list(last.values()) + share:
-        copy.wait_send()
-    for key, copy in ring.items():
-        if key[2] != "at":
-            copy.wait_send()
-    for copies in (pr0, pr1, sq0, sq1, nm0, nm1):
-        for copy, _, _ in copies:
-            copy.wait_send()
+    def left(size_of, sem):
+        pltpu.make_async_copy(size_of, size_of, sem).wait()
+
+    left(W.at[0, 0, pl.ds(0, 3)], ag_s.at[0])
+    left(W.at[0, pl.ds(0, 3)], ag_s.at[1])
+    left(W.at[0], fw_s.at[0])
+    left(T, ex_s.at[0])
+    for k in range(4):
+        left(D[k].at[pl.ds(0, 3)], rs_s.at[0, k])
+        left(E[k].at[pl.ds(0, 3)], rs_s.at[1, k])
+        left(F[k].at[pl.ds(0, 3)], p3_s.at[k])
+    left(GA.at[pl.ds(0, 3)], gz_s.at[0])
+    for i, buf in enumerate((prc, prp, sqc, sqp, nmc, nmp)):
+        left(buf.at[pl.ds(0, buf.shape[0] - 1)], sm_s.at[i])
 
 
 def write_out(acc, ig, up, ln, rn, inv, lo_out, ig_out, up_out, ln_out, rn_out, lo, sems):
@@ -507,28 +539,20 @@
             vm((8, 8, 128), F32),
             vm((16, 8, 128), F32),
             vm((1, 8, 128), F32),
-            dma((5, 4)),
-            dma((5, 4)),
+            dma((2,)),
+            dma((5, 3)),
+            dma((1,)),
+            dma((7,)),
+            dma((1,)),
+            dma((8,)),
+            dma((2, 4)),
+            dma((2, 4, 3)),
             dma((4,)),
             dma((4,)),
-            dma((8,)),
-            dma((8,)),
-            dma((2, 4, 6)),
-            dma((2, 4, 6)),
-            dma((4, 3)),
-            dma((4, 3)),
-            dma((3,)),
-            dma((3,)),
-            dma((2,)),
-            dma((2,)),
-            dma((15,)),
-            dma((15,)),
-            dma((15,)),
-            dma((15,)),
-            dma((7,)),
-            dma((7,)),
-            dma((15,)),
-            dma((15,)),
+            dma((1,)),
+            dma((1,)),
+            dma((6,)),
+            dma((6,)),
             dma,
             dma,
             dma((2, 4)),

time: 101 us -> 93.5 us (0.926)
  Pallas kernels: 101 us -> 92.6 us
    pallas_call x1, Pallas kernels: 97.8 us -> 89.7 us  [per_device(): pl.pallas_call(kernel, out_shape=(vm((512, 2048), F32), vm((512, 4096), B...]
where the time goes in v3:
time: 93.5 us; the launch traced here: 93.2 us
  Pallas kernels  92.6 us (99%)
    pallas_call x1, Pallas kernels, per_device(): pl.pallas_call(kernel, out_shape=(vm((512, 2048), F32), vm((512, 4096), B...  89.7 us
    pallas_call x1, Pallas kernels, per_device(): pl.pallas_call(write_out, out_shape=(jax.ShapeDtypeStruct((512, 2048), BF...  2.88 us

profile of v3, /device:TPU:1, one launch (start us, length us, event | category | flops | bytes accessed | tf_op | source)
XLA Modules:
  0.0 93.2 jit_solution(2456095381058220883)
XLA Ops:
  0.6 89.7 %shard_map.83 = (f32[512,2048]{1,0:T(8,128)S(1)}, bf16[512,4096]{1,0:T(8,128)(2,1)S(1)}, bf16[128,2048]{1,0:T(8,128)(2,1)S(1)}, f32[1,128]{1,0:T(1,128)S(1)}, f3...) custom-call(bf16[512,4096]{1,0:T(8,128)(2,1)} %tok.1, bf16[512,2048]{1,0:T(8,128)(2,1)} %cot.1, bf16[128,2048]{1,0:T(8,128)(2,1)} %w.1, ...), custom_call_target="tpu_custom_call" | custom-call | tf_op jit(solution)/shard_map/pallas_call | solution.py:511
  90.3 2.9 %shard_map.84 = (bf16[512,2048]{1,0:T(8,128)(2,1)}, bf16[512,4096]{1,0:T(8,128)(2,1)}, bf16[128,2048]{1,0:T(8,128)(2,1)}, f32[1,128]{1,0:T(1,128)}, f32[1,2048]{1,0:T(1,128)}) custom-call(f32[512,2048]{1,0:T(8,128)S(1)} %get-tuple-element.16.acc, bf16[512,4096]{1,0:T(8,128)(2,1)S(1)} %get-tuple-element.17.ig, bf16[128,2048]{1,0:T(8,128)(2,1)S(1)} %get-tuple-element.18.up, ...), custom_call_target="tpu_custom_call" | custom-call | tf_op jit(solution)/shard_map/pallas_call | solution.py:564

commit v4 on v3

--- a/solution.py
+++ b/solution.py
@@ -76,12 +76,14 @@
             col = (m1 + OFFSET[op - 1]) % 4
             at = lambda step, rows=whole, col=col: W.at[mc, col, (m2 + step) % 4, rows]
             dev = along2
-        src = (at(0), at(0), at(3, top), at(1, bottom))
-        got = (at(3), at(1))
-        for e, step in enumerate((1, 3, 1, 3)):
-            gather[op, e] = copy_to(src[e], src[e], ag_s.at[min(op, 1)], ag_r.at[op, min(e, 2)], dev(step))
-        landed[op, 0], landed[op, 1] = (got[0], ag_r.at[op, 0]), (got[1], ag_r.at[op, 1])
-        landed[op, 2] = (at(2), ag_r.at[op, 2])
+        moves = (
+            (at(0, top), 1, 0), (at(0, bottom), 3, 1), (at(0, bottom), 1, 3), (at(0, top), 3, 4),
+            (at(3, top), 1, 2), (at(1, bottom), 3, 2),
+        )
+        for e, (src, step, r) in enumerate(moves):
+            gather[op, e] = copy_to(src, src, ag_s.at[min(op, 1)], ag_r.at[op, r], dev(step))
+        for r, got in enumerate((at(3, top), at(1, bottom), at(2), at(3, bottom), at(1, top))):
+            landed[op, r] = (got, ag_r.at[op, r])
     partner = peer("fc", 1)
     across, crossed = [], []
     for slot in range(3):
@@ -191,20 +193,34 @@
     pl.semaphore_wait(barrier, len(others))
 
     def spread(op):
-        gather[op, 0].start()
-        gather[op, 1].start()
+        if op == 2:
+            arrived(*landed[0, 4])
+        elif op == 3:
+            arrived(*landed[0, 3])
+        elif op == 4:
+            arrived(*landed[0, 2])
+        for e in range(2):
+            gather[op, e].start()
+        if op != 4:
+            spread_rest(op)
+
+    def spread_rest(op):
+        for e in (2, 3):
+            gather[op, e].start()
 
     def forward(op):
-        arrived(*landed[op, 0])
-        gather[op, 2].start()
-        arrived(*landed[op, 1])
-        gather[op, 3].start()
+        for e in range(2):
+            arrived(*landed[op, e])
+            gather[op, 4 + e].start()
 
     def cross(slot):
-        arrived(*landed[slot + 1, 2])
+        for e in (2, 3, 4):
+            arrived(*landed[slot + 1, e])
         across[slot].start()
 
     def cross_first():
+        for e in (3, 4):
+            arrived(*landed[4, e])
         for i in (3, 4, 5):
             across[i].start()
 
@@ -212,14 +228,8 @@
         arrived(*landed[4, 2])
         across[6].start()
 
-    def meet():
-        arrived(*landed[0, 2])
-
     for copy in pr0[0]:
         copy.start()
-    put(pr1, prp, mx * 4 + my, total(pr0, prc))
-    spread(0)
-    spread(1)
     load_c.wait()
     give_c[0].start()
     for g in range(4):
@@ -227,6 +237,9 @@
         give_t[g].start()
     for copy in give_c[1:]:
         copy.start()
+    put(pr1, prp, here, total(pr0, prc))
+    spread(0)
+    spread(1)
 
     def ring_go(ph, k, *events):
         for e in events:
@@ -240,6 +253,18 @@
             for i in range(2):
                 S[k][t, lo_ + i] = (S[k][t, lo_ + i].astype(F32) + A1[k][d, i].astype(F32)).astype(BF)
             ring[ph, k, e].start()
+
+    def mid_first():
+        for k in range(2):
+            @pl.when(mc == k)
+            def _():
+                ring_mid(1, k)
+
+    def mid_second():
+        for k in range(2):
+            @pl.when(mc == 1 - k)
+            def _():
+                ring_mid(1, k)
 
     def ring_end(ph, k):
         S, A2, out = ((D, R2, E), (E, Q2, F))[ph]
@@ -325,8 +350,8 @@
         3: [(ring_go, 0, 0, 0, 1), (ring_go, 0, 1, 0, 1)],
         5: [(sq_start,)],
         7: [(ring_go, 0, 0, 2), (ring_go, 0, 1, 2), (sq_plane,)],
-        11: [(forward, 1), (forward, 0), (spread, 2)],
-        14: [(sq_end,)],
+        8: [(forward, 1), (forward, 0)],
+        12: [(spread, 2)],
         15: [
             (ring_go, 0, 2, 0, 1, 2, 3), (ring_go, 0, 3, 0, 1, 2, 3),
             (ring_go, 0, 0, 3), (ring_go, 0, 1, 3),
@@ -395,17 +420,16 @@
 
     BOTH_EVENTS = {
         0: [(cross, 0)],
+        1: [(sq_end,)],
         2: [(group, 0)],
-        3: [(ring_mid, 0, 0), (ring_mid, 0, 1)],
-        4: [(forward, 2), (ring_mid, 0, 2), (ring_mid, 0, 3), (spread, 3), (meet,), (cross, 1)],
+        3: [(ring_mid, 0, 0), (ring_mid, 0, 1), (forward, 2)],
+        4: [(ring_mid, 0, 2), (ring_mid, 0, 3), (spread, 3), (cross, 1)],
         6: [(group, 1)],
-        7: [(p1_end, 2), (p1_end, 3)],
-        8: [
-            (p1_end, 0), (p1_end, 1), (forward, 3),
-            (ring_mid, 1, 2), (ring_mid, 1, 3), (ring_mid, 1, 0), (ring_mid, 1, 1),
-            (spread, 4), (cross, 2),
-        ],
-        10: [(p2_end, 2), (p2_end, 3), (p2_end, 0), (p2_end, 1), (group, 2)],
+        7: [(forward, 3), (p1_end, 2), (p1_end, 3)],
+        8: [(p1_end, 0), (p1_end, 1), (ring_mid, 1, 2), (ring_mid, 1, 3), (mid_first,), (cross, 2)],
+        9: [(mid_second,), (spread, 4), (p2_end, 2), (p2_end, 3)],
+        10: [(p2_end, 0), (p2_end, 1), (spread_rest, 4), (group, 2)],
+        11: [(forward, 4)],
     }
     lax.fori_loop(0, 12, both, 0)
 
@@ -441,9 +465,10 @@
         return carry
 
     HALF_EVENTS = {
-        0: [(forward, 4), (cross_first,)],
-        2: [(norms,), (group, 3), (group, 4)],
-        4: [(nm_plane,), (cross_last,)],
+        0: [(norms,), (cross_first,)],
+        1: [(nm_plane,)],
+        2: [(group, 3), (group, 4)],
+        4: [(cross_last,)],
         6: [(group, 5), (group, 6)],
     }
     lax.fori_loop(0, 8, halves, 0)
@@ -540,7 +565,7 @@
             vm((16, 8, 128), F32),
             vm((1, 8, 128), F32),
             dma((2,)),
-            dma((5, 3)),
+            dma((5, 5)),
             dma((1,)),
             dma((7,)),
             dma((1,)),

time: 93.5 us -> 90.4 us (0.967)
  Pallas kernels: 92.6 us -> 89.6 us
    pallas_call x1, Pallas kernels: 89.7 us -> 86.7 us  [per_device(): pl.pallas_call(kernel, out_shape=(vm((512, 2048), F32), vm((512, 4096), B...]
where the time goes in v4:
time: 90.4 us; the launch traced here: 90.3 us
  Pallas kernels  89.6 us (99%)
    pallas_call x1, Pallas kernels, per_device(): pl.pallas_call(kernel, out_shape=(vm((512, 2048), F32), vm((512, 4096), B...  86.7 us
    pallas_call x1, Pallas kernels, per_device(): pl.pallas_call(write_out, out_shape=(jax.ShapeDtypeStruct((512, 2048), BF...  2.88 us

profile of v4, /device:TPU:1, one launch (start us, length us, event | category | flops | bytes accessed | tf_op | source)
XLA Modules:
  0.0 90.3 jit_solution(6284272589026747421)
XLA Ops:
  0.6 86.7 %shard_map.83 = (f32[512,2048]{1,0:T(8,128)S(1)}, bf16[512,4096]{1,0:T(8,128)(2,1)S(1)}, bf16[128,2048]{1,0:T(8,128)(2,1)S(1)}, f32[1,128]{1,0:T(1,128)S(1)}, f3...) custom-call(bf16[512,4096]{1,0:T(8,128)(2,1)} %tok.1, bf16[512,2048]{1,0:T(8,128)(2,1)} %cot.1, bf16[128,2048]{1,0:T(8,128)(2,1)} %w.1, ...), custom_call_target="tpu_custom_call" | custom-call | tf_op jit(solution)/shard_map/pallas_call | solution.py:536
  87.4 2.9 %shard_map.84 = (bf16[512,2048]{1,0:T(8,128)(2,1)}, bf16[512,4096]{1,0:T(8,128)(2,1)}, bf16[128,2048]{1,0:T(8,128)(2,1)}, f32[1,128]{1,0:T(1,128)}, f32[1,2048]{1,0:T(1,128)}) custom-call(f32[512,2048]{1,0:T(8,128)S(1)} %get-tuple-element.16.acc, bf16[512,4096]{1,0:T(8,128)(2,1)S(1)} %get-tuple-element.17.ig, bf16[128,2048]{1,0:T(8,128)(2,1)S(1)} %get-tuple-element.18.up, ...), custom_call_target="tpu_custom_call" | custom-call | tf_op jit(solution)/shard_map/pallas_call | solution.py:589

commit v5 on v4

--- a/solution.py
+++ b/solution.py
@@ -201,7 +201,7 @@
             arrived(*landed[0, 2])
         for e in range(2):
             gather[op, e].start()
-        if op != 4:
+        if op < 3:
             spread_rest(op)
 
     def spread_rest(op):
@@ -254,17 +254,17 @@
                 S[k][t, lo_ + i] = (S[k][t, lo_ + i].astype(F32) + A1[k][d, i].astype(F32)).astype(BF)
             ring[ph, k, e].start()
 
-    def mid_first():
+    def mid_first(ph, k0):
         for k in range(2):
             @pl.when(mc == k)
             def _():
-                ring_mid(1, k)
-
-    def mid_second():
+                ring_mid(ph, k0 + k)
+
+    def mid_second(ph, k0):
         for k in range(2):
             @pl.when(mc == 1 - k)
             def _():
-                ring_mid(1, k)
+                ring_mid(ph, k0 + k)
 
     def ring_end(ph, k):
         S, A2, out = ((D, R2, E), (E, Q2, F))[ph]
@@ -351,7 +351,7 @@
         5: [(sq_start,)],
         7: [(ring_go, 0, 0, 2), (ring_go, 0, 1, 2), (sq_plane,)],
         8: [(forward, 1), (forward, 0)],
-        12: [(spread, 2)],
+        11: [(spread, 2)],
         15: [
             (ring_go, 0, 2, 0, 1, 2, 3), (ring_go, 0, 3, 0, 1, 2, 3),
             (ring_go, 0, 0, 3), (ring_go, 0, 1, 3),
@@ -423,11 +423,11 @@
         1: [(sq_end,)],
         2: [(group, 0)],
         3: [(ring_mid, 0, 0), (ring_mid, 0, 1), (forward, 2)],
-        4: [(ring_mid, 0, 2), (ring_mid, 0, 3), (spread, 3), (cross, 1)],
+        4: [(mid_first, 0, 2), (spread, 3), (mid_second, 0, 2), (spread_rest, 3), (cross, 1)],
         6: [(group, 1)],
         7: [(forward, 3), (p1_end, 2), (p1_end, 3)],
-        8: [(p1_end, 0), (p1_end, 1), (ring_mid, 1, 2), (ring_mid, 1, 3), (mid_first,), (cross, 2)],
-        9: [(mid_second,), (spread, 4), (p2_end, 2), (p2_end, 3)],
+        8: [(p1_end, 0), (p1_end, 1), (ring_mid, 1, 2), (ring_mid, 1, 3), (mid_first, 1, 0), (cross, 2)],
+        9: [(mid_second, 1, 0), (spread, 4), (p2_end, 2), (p2_end, 3)],
         10: [(p2_end, 0), (p2_end, 1), (spread_rest, 4), (group, 2)],
         11: [(forward, 4)],
     }
@@ -466,8 +466,7 @@
 
     HALF_EVENTS = {
         0: [(norms,), (cross_first,)],
-        1: [(nm_plane,)],
-        2: [(group, 3), (group, 4)],
+        2: [(nm_plane,), (group, 3), (group, 4)],
         4: [(cross_last,)],
         6: [(group, 5), (group, 6)],
     }

time: 90.4 us -> 89.6 us (level)
  no operation moved by 1% of the time
where the time goes in v5:
time: 89.6 us; the launch traced here: 89.5 us
  Pallas kernels  88.8 us (99%)
    pallas_call x1, Pallas kernels, per_device(): pl.pallas_call(kernel, out_shape=(vm((512, 2048), F32), vm((512, 4096), B...  85.9 us
    pallas_call x1, Pallas kernels, per_device(): pl.pallas_call(write_out, out_shape=(jax.ShapeDtypeStruct((512, 2048), BF...  2.88 us

profile of v5, /device:TPU:1, one launch (start us, length us, event | category | flops | bytes accessed | tf_op | source)
XLA Modules:
  0.0 89.5 jit_solution(4548939645102828473)
XLA Ops:
  0.6 85.9 %shard_map.83 = (f32[512,2048]{1,0:T(8,128)S(1)}, bf16[512,4096]{1,0:T(8,128)(2,1)S(1)}, bf16[128,2048]{1,0:T(8,128)(2,1)S(1)}, f32[1,128]{1,0:T(1,128)S(1)}, f3...) custom-call(bf16[512,4096]{1,0:T(8,128)(2,1)} %tok.1, bf16[512,2048]{1,0:T(8,128)(2,1)} %cot.1, bf16[128,2048]{1,0:T(8,128)(2,1)} %w.1, ...), custom_call_target="tpu_custom_call" | custom-call | tf_op jit(solution)/shard_map/pallas_call | solution.py:535
  86.6 2.9 %shard_map.84 = (bf16[512,2048]{1,0:T(8,128)(2,1)}, bf16[512,4096]{1,0:T(8,128)(2,1)}, bf16[128,2048]{1,0:T(8,128)(2,1)}, f32[1,128]{1,0:T(1,128)}, f32[1,2048]{1,0:T(1,128)}) custom-call(f32[512,2048]{1,0:T(8,128)S(1)} %get-tuple-element.16.acc, bf16[512,4096]{1,0:T(8,128)(2,1)S(1)} %get-tuple-element.17.ig, bf16[128,2048]{1,0:T(8,128)(2,1)S(1)} %get-tuple-element.18.up, ...), custom_call_target="tpu_custom_call" | custom-call | tf_op jit(solution)/shard_map/pallas_call | solution.py:588
